TPU v7x, 512 devices: a whole 4x8x8 slice. The times are simulated.
512 devices in a mesh: seq: 64 (over z, x, core), mp: 8 (over y).
Axes of the slice: x: 4, y: 8, z: 8, core: 2. Of those that a mesh axis runs over, the one named last changes fastest.
Arguments:
- x_inner: bfloat16 [2, 16384, 5120], P(None, 'seq', 'mp'), may hold values from -6 to 6
- z_gate: bfloat16 [2, 16384, 5120], P(None, 'seq', 'mp'), may hold values from -6 to 6
- b_input: bfloat16 [2, 16384, 128], P(None, 'seq'), may hold values from -6 to 6
- c_input: bfloat16 [2, 16384, 128], P(None, 'seq'), may hold values from -6 to 6
- dt_raw: float32 [2, 16384, 80], P(None, 'seq', 'mp'), may hold values from -3 to 3
- doc_ids: int32 [2, 16384], P(None, 'seq'), may hold values from 0 to 2, never falling along the last dimension, each value on 1 to 8192 neighbouring positions
- conv_x: bfloat16 [4, 5120], P(None, 'mp'), may hold values from -3 to 3
- conv_b: bfloat16 [4, 128], replicated, may hold values from -3 to 3
- conv_c: bfloat16 [4, 128], replicated, may hold values from -3 to 3
- dt_bias: float32 [80], P('mp'), as said below
- decay_rate: float32 [80], P('mp'), may hold values from 0.0625 to 0.25
- norm_gain: float32 [5120], P('mp'), may hold values from 0.25 to 1.75
- w_out: bfloat16 [5120, 2560], P('mp'), may hold values from -0.078125 to 0.078125
Outputs:
- layer_out: bfloat16 [2, 16384, 2560], P(None, 'seq', 'mp')
Inputs may be any that keep to these rules, and one draw needn't show every extreme that they name: `doc_ids`: in each sequence the document numbers start at 0, never fall and rise by one at each new document; there are three documents, the longest exactly 8192 positions. `dt_bias`: softplus of each entry lies between 8/16384 and 1.
All inputs are finite; a program needn't handle non-finite values.
Results may differ from a plain program's by a relative error of at most 0.02.
Values may be sent and summed in bfloat16 or wider, within the bound.
A program may use at most 128 MiB of HBM per device.

v0:
```python
import jax
import jax.numpy as jnp
from jax import lax
from jax.sharding import Mesh
from jax.sharding import PartitionSpec as P

BLOCK = 256
INNER = 5120
SEQ = ("seq_0", "seq_1", "seq_2")


EPSILON = 1e-05


def passed_along(value, axis, steps):
    count = lax.axis_size(axis)
    first, last = max(0, -steps), min(count, count - steps)
    return lax.ppermute(value, axis, [(source, source + steps) for source in range(first, last)])


def nothing_yet(x, identity):
    return jax.tree.map(
        lambda part, zero: jnp.zeros_like(part) + jnp.asarray(zero, part.dtype), x, identity
    )


def carried_in(x, axes, combine, identity, reverse):
    before = start = nothing_yet(x, identity)
    total = x
    for axis in reversed(axes):
        peers, mine = lax.axis_size(axis), lax.axis_index(axis)
        pieces = jax.tree.map(lambda part: lax.all_gather(part, axis), total)
        inside, total = start, start
        for k in reversed(range(peers)) if reverse else range(peers):
            passed = k > mine if reverse else k < mine
            total = combine(total, jax.tree.map(lambda part: part[k], pieces))
            inside = jax.tree.map(lambda new, old: jnp.where(passed, new, old), total, inside)
        before = combine(inside, before)
    return before


def causal_conv(window, marks, weight, length):
    taps = weight.shape[0]
    current = marks[:, taps - 1 :]
    total = jnp.zeros((window.shape[0], length, window.shape[2]), jnp.float32)
    for offset in range(taps):
        same = (marks[:, offset : offset + length] == current)[:, :, None]
        term = window[:, offset : offset + length].astype(jnp.float32) * weight[offset].astype(
            jnp.float32
        )
        total = total + jnp.where(same, term, 0.0)
    return jax.nn.silu(total).astype(jnp.bfloat16)


def combine_states(earlier, later):
    return (earlier[0] * later[0], later[0][:, :, None, None] * earlier[1] + later[1])


def block_terms(xs, bs, cs, steps, logs, docs, before):
    width = docs.shape[1]
    order = jnp.arange(width)
    causal = order[:, None] >= order[None, :]
    masked = causal[None] & (docs[:, :, None] == docs[:, None, :])
    scores = jnp.einsum("btn,bsn->bts", cs, bs, preferred_element_type=jnp.float32)
    spread = jnp.where(masked[:, :, :, None], logs[:, :, None, :] - logs[:, None, :, :], 0.0)
    mixing = jnp.where(
        masked[:, :, :, None], scores[:, :, :, None] * jnp.exp(spread) * steps[:, None, :, :], 0.0
    ).astype(jnp.bfloat16)
    inner = jnp.einsum("btsh,bshp->bthp", mixing, xs, preferred_element_type=jnp.float32)
    keeps = (docs == docs[:, -1:])[:, :, None]
    weights = jnp.where(keeps, jnp.exp(logs[:, -1:, :] - logs) * steps, 0.0)
    loaded = (weights[:, :, :, None] * bs[:, :, None, :].astype(jnp.float32)).astype(jnp.bfloat16)
    fresh = jnp.einsum("bshp,bshn->bhpn", xs, loaded, preferred_element_type=jnp.float32)
    carried = docs == before[:, None]
    entry = jnp.where(carried[:, :, None], jnp.exp(logs), 0.0)
    return (inner, fresh, entry, entry[:, -1, :])


def front_work(xs, bs, cs, steps, docs, before, rates):
    pieces = []
    running = jnp.zeros((xs.shape[0], xs.shape[2], xs.shape[3], bs.shape[2]), jnp.float32)
    product = jnp.ones((xs.shape[0], xs.shape[2]), jnp.float32)
    prior = before
    for index in range(xs.shape[1] // BLOCK):
        lower = index * BLOCK
        upper = lower + BLOCK
        steps_here = steps[:, lower:upper]
        logs = jnp.cumsum(-(steps_here * rates), axis=1)
        docs_here = docs[:, lower:upper]
        inner, fresh, entry, gate = block_terms(
            xs[:, lower:upper],
            bs[:, lower:upper],
            cs[:, lower:upper],
            steps_here,
            logs,
            docs_here,
            prior,
        )
        pieces.append((inner, entry, running, product))
        running = gate[:, :, None, None] * running + fresh
        product = product * gate
        prior = docs_here[:, -1]
    return (pieces, product, running)


def back_work(pieces, incoming, cs):
    outputs = []
    for index, piece in enumerate(pieces):
        inner, entry, running, product = piece
        entering = (product[:, :, None, None] * incoming + running).astype(jnp.bfloat16)
        cs_here = cs[:, index * BLOCK : (index + 1) * BLOCK]
        outer = jnp.einsum("btn,bhpn->bthp", cs_here, entering, preferred_element_type=jnp.float32)
        outputs.append(inner + entry[:, :, :, None] * outer)
    return jnp.concatenate(outputs, axis=1)


def shards(
    x_inner,
    z_gate,
    b_input,
    c_input,
    dt_raw,
    doc_ids,
    conv_x,
    conv_b,
    conv_c,
    dt_bias,
    decay_rate,
    norm_gain,
    w_out,
):
    batch, length, channels = x_inner.shape
    heads = dt_raw.shape[2]
    state_dim = b_input.shape[2]
    edge = conv_x.shape[0] - 1
    tail = jnp.concatenate(
        [x_inner[:, length - edge :], b_input[:, length - edge :], c_input[:, length - edge :]],
        axis=2,
    )
    tail_docs = doc_ids[:, length - edge :]
    packed = jnp.concatenate([tail, (tail_docs + 1).astype(jnp.bfloat16)[:, :, None]], axis=2)
    moved = passed_along(packed, SEQ, 1)
    halo_rows = moved[:, :, :-1]
    halo_docs = moved[:, :, -1].astype(jnp.int32) - 1
    marks = jnp.concatenate([halo_docs, doc_ids], axis=1)
    x_conv = causal_conv(
        jnp.concatenate([halo_rows[:, :, :channels], x_inner], axis=1), marks, conv_x, length
    )
    b_conv = causal_conv(
        jnp.concatenate([halo_rows[:, :, channels : channels + state_dim], b_input], axis=1),
        marks,
        conv_b,
        length,
    )
    c_conv = causal_conv(
        jnp.concatenate([halo_rows[:, :, channels + state_dim :], c_input], axis=1),
        marks,
        conv_c,
        length,
    )
    steps = jax.nn.softplus(dt_raw + dt_bias)
    xs = x_conv.reshape(batch, length, heads, channels // heads)
    before = halo_docs[:, -1]
    pieces, product, running = front_work(xs, b_conv, c_conv, steps, doc_ids, before, decay_rate)
    identity = (jnp.ones_like(product), jnp.zeros_like(running))
    prefix = tuple(
        (
            part.astype(kind)
            for part, kind in zip(
                carried_in(
                    (product.astype(jnp.bfloat16), running.astype(jnp.bfloat16)),
                    SEQ,
                    combine_states,
                    identity,
                    False,
                ),
                (jnp.float32, jnp.float32),
            )
        )
    )
    mixed_y = back_work(pieces, prefix[1], c_conv)
    gated = mixed_y.reshape(batch, length, channels) * jax.nn.silu(z_gate.astype(jnp.float32))
    squares = lax.psum(jnp.sum(gated * gated, axis=2), "mp")
    scale = lax.rsqrt(squares / INNER + EPSILON)
    normed = (gated * scale[:, :, None] * norm_gain).astype(jnp.bfloat16)
    flat = normed.reshape(batch * length, channels)
    width_out = w_out.shape[1] // lax.axis_size("mp")

    def project():
        columns = w_out
        return lax.dot_general(
            columns, flat, (((0,), (1,)), ((), ())), preferred_element_type=jnp.float32
        )

    summed = lax.psum_scatter(
        project().astype(jnp.bfloat16), "mp", scatter_dimension=0, tiled=True
    ).astype(jnp.float32)
    return summed.T.reshape(batch, length, width_out).astype(jnp.bfloat16)


def solution(mesh):
    torus = Mesh(mesh.devices.reshape(8, 4, 2, mesh.shape["mp"]), ("seq_0", "seq_1", "seq_2", "mp"))
    placed = (
        P(None, SEQ, "mp"),
        P(None, SEQ, "mp"),
        P(None, SEQ, None),
        P(None, SEQ, None),
        P(None, SEQ, "mp"),
        P(None, SEQ),
        P(None, "mp"),
        P(),
        P(),
        P("mp"),
        P("mp"),
        P("mp"),
        P("mp", None),
    )
    return jax.shard_map(
        shards, mesh=torus, in_specs=placed, out_specs=P(None, SEQ, "mp"), check_vma=False
    )
```

profile of v0, /device:TPU:2, one launch (start us, length us, event | category | flops | bytes accessed | tf_op | source)
XLA Modules:
  0.0 239.3 jit_solution(978247398494687100)
XLA Ops:
  6.5 0.9 fusion.119
  7.5 0.8 slice.210
  10.0 0.9 copy.158
  10.9 1.9 pad_maximum_fusion.1
  12.8 1.9 collective-permute-start
  15.3 0.9 copy.166
  16.2 2.3 multiply_negate_fusion
  19.2 2.2 reduce-window.6
  22.4 0.9 copy.182
  23.3 1.4 bitcast_convert_fusion.3
  26.1 2.2 copy.162
  29.1 1.3 fusion.115
  30.4 1.4 copy.176
  31.9 1.4 copy.173
  33.2 3.1 %multiply_select_fusion = (f32[2,256,10]{2,0,1:T(2,128)}, f32[2,256,10]{2,0,1:T(2,128)S(1)}) fusion(f32[2,256,10]{2,0,1:T(2,128)} %get-tuple-element.18, pred[2,256]{0,1:T(8,128)(4,1)} %copy.176, f32[2,10]{1,0:T(2,128)} %slice_bitcast_fusion.8, f32[2,10,2,128]{1,0,3,2:T(2,128)S(1)} %copy.182, pred[2,256]{0,1:T(8,128)(4,1)} %copy.173), kind=kLoop, calls=%fused_computation.113 | loop fusion | flops 20480 | bytes 83024 | tf_op jit(solution)/shard_map/jit(_where)/select_n | solution.py:71
  37.6 1.5 fusion.124
  39.1 1.5 copy.165
  40.6 1.7 copy.177
  43.0 2.1 fusion.123
  45.0 1.0 slice.285
  46.1 2.3 multiply_convert_fusion.3
  48.4 1.2 fusion.18
  49.6 3.5 %all-gather.1 = bf16[4,10,64,128]{3,2,1,0:T(8,128)(2,1)S(1)} all-gather(bf16[2,10,64,128]{3,2,1,0:T(8,128)(2,1)S(1)} %fusion.18), channel_id=3, replica_groups=mesh['seq_0'=8,'seq_1'=4,'seq_2'=2,'mp'=8] {'seq_2'}, dimensions={0}, use_global_device_ids=true | all-gather | bytes 983040 | tf_op jit(solution)/shard_map/all_gather | solution.py:32
  53.1 1.8 all-gather
  54.9 11.7 %all-gather.2 = bf16[8,1,10]{2,1,0:T(2,128)(2,1)S(1)} all-gather(bf16[2,1,10]{2,1,0:T(2,128)(2,1)S(1)} %get-tuple-element.40), channel_id=4, replica_groups=mesh['seq_0'=8,'seq_1'=4,'seq_2'=2,'mp'=8] {'seq_1'}, dimensions={0}, use_global_device_ids=true | all-gather | bytes 200 | tf_op jit(solution)/shard_map/all_gather | solution.py:32
  68.4 0.9 bitcast_add_fusion.4
  69.3 29.9 %all-gather.6.cloned.1.call-done = bf16[4,2,10,64,128]{4,3,2,1,0:T(8,128)(2,1)} async-done(((bf16[1,2,10,64,128]{4,3,2,1,0:T(8,128)(2,1)}), bf16[4,2,10,64,128]{4,3,2,1,0:T(8,128)(2,1)}) %all-gather.6.cloned.1.call-update) | async-done | bytes 1310736 | tf_op jit(solution)/shard_map/all_gather | solution.py:32
  99.2 2.2 multiply_add_fusion
  101.5 1.7 copy.172
  103.8 2.2 copy.178
  106.1 1.4 bitcast_convert_fusion.7
  107.5 0.8 compare_and_fusion
  109.0 0.9 copy.164
  110.6 17.3 %all_gather.28 = bf16[8,2,10]{2,1,0:T(2,128)(2,1)S(1)} all-gather(bf16[1,2,10]{2,1,0:T(2,128)(2,1)S(1)} %bitcast.213), channel_id=1, replica_groups=mesh['seq_0'=8,'seq_1'=4,'seq_2'=2,'mp'=8] {'seq_0'}, dimensions={0}, use_global_device_ids=true | all-gather | bytes 360 | tf_op jit(solution)/shard_map/all_gather | solution.py:32
  128.0 1.5 multiply_convert_fusion.9
  129.5 1.1 fusion.126
  130.8 3.9 %fusion.9 = f32[2,256,10,64]{1,3,2,0:T(8,128)} fusion(bf16[2,256,10,64]{1,3,2,0:T(8,128)(2,1)} %bitcast.209, f32[2,256,10]{1,2,0:T(8,128)} %copy.172, f32[2,256,10]{1,2,0:T(8,128)} %copy.170, f32[2,256,256]{2,1,0:T(8,128)S(1)} %fusion.126, pred[2,256,256]{2,1,0:T(8,128)(4,1)} %compare_and_fusion), kind=kOutput, calls=%fused_computation.15 | convolution fusion | flops 175636480 | bytes 2662400 | tf_op jit(solution)/shard_map/btsh,bshp->bthp/dot_general | solution.py:69
  134.7 13.9 %all-gather.8.cloned.1.call-done = bf16[8,2,10,64,128]{4,3,2,1,0:T(8,128)(2,1)} async-done(((bf16[1,2,10,64,128]{4,3,2,1,0:T(8,128)(2,1)}), bf16[8,2,10,64,128]{4,3,2,1,0:T(8,128)(2,1)}) %all-gather.8.cloned.1.call-update) | async-done | bytes 2621456 | tf_op jit(solution)/shard_map/all_gather | solution.py:32
  148.6 4.4 %fusion.8 = f32[2,256,10,64]{1,3,2,0:T(8,128)S(1)} fusion(f32[2,256,10,64]{1,3,2,0:T(8,128)} %fusion.9, f32[2,256,10]{1,2,0:T(8,128)S(1)} %copy-done.8, bf16[8,2,10,64,128]{4,3,2,1,0:T(8,128)(2,1)} %all-gather.8.cloned.1.call-done, pred[]{:T(512)S(6)} %gt.47, pred[]{:T(512)S(6)} %gt.46, pred[]{:T(512)S(6)} %gt.45, pred[]{:T(512)S(6)} %gt.44, pred[]{:T(512)S(6)} %gt.43, ...), kind=kOutput, calls=%fused_computation.14 | convolution fusion | flops 99450880 | bytes 7361166 | tf_op jit(solution)/shard_map/btn,bhpn->bthp/dot_general | solution.py:112
  153.0 1.1 copy-done.2
  154.6 17.2 %psum.7 = f32[2,256]{1,0:T(2,128)S(1)} all-reduce(f32[2,256]{1,0:T(2,128)S(1)} %multiply_reduce_fusion), channel_id=1, replica_groups=mesh['seq_0'=8,'seq_1'=4,'seq_2'=2,'mp'=8] {'mp'}, use_global_device_ids=true, to_apply=%region_3.4 | all-reduce | flops 512 | bytes 4096 | tf_op jit(solution)/shard_map/psum | solution.py:183
  171.8 2.8 %multiply_convert_fusion.2 = bf16[2,256,640]{1,2,0:T(8,128)(2,1)} fusion(f32[640]{0:T(1024)S(1)} %copy-done.16, f32[2,256]{1,0:T(2,128)S(1)} %add_rsqrt_fusion, bf16[2,256,640]{1,2,0:T(8,128)(2,1)} %copy.178, f32[2,256,10,64]{1,3,2,0:T(8,128)} %copy-done.2), kind=kLoop, calls=%fused_computation.21 | loop fusion | flops 2949120 | bytes 2626048 | tf_op jit(solution)/shard_map/convert_element_type | solution.py:185
  174.6 2.2 copy.179
  176.8 4.8 %fusion = bf16[2560,512]{0,1:T(8,128)(2,1)} fusion(bf16[512,640]{1,0:T(8,128)(2,1)} %bitcast.210, bf16[640,2560]{1,0:T(8,128)(2,1)S(1)} %copy-done), kind=kOutput, calls=%fused_computation.2 | convolution fusion | flops 1679032320 | bytes 6553600 | tf_op jit(solution)/shard_map/dot_general | solution.py:191
  181.6 4.4 %copy.184 = bf16[2560,512]{1,0:T(8,128)(2,1)} copy(bf16[2560,512]{0,1:T(8,128)(2,1)} %fusion) | data formatting | bytes 5242880
  186.0 43.0 %reduce-scatter.4.cloned.1.call-done = bf16[320,512]{1,0:T(8,128)(2,1)} async-done(((bf16[2560,512]{1,0:T(8,128)(2,1)}), bf16[320,512]{1,0:T(8,128)(2,1)}) %reduce-scatter.4.cloned.1.call-update) | async-done | bytes 327696
  229.0 1.9 copy.185
  230.9 1.9 copy.180
  (96 shorter events, 12.7 us)
Async XLA Ops:
  6.5 170.2 %copy-start = (bf16[640,2560]{1,0:T(8,128)(2,1)S(1)}, bf16[640,2560]{1,0:T(8,128)(2,1)}, u32[]{:S(2)}) copy-start(bf16[640,2560]{1,0:T(8,128)(2,1)} %param.25) | copy-start | bytes 9830404
  6.5 8.2 %copy-start.11 = (bf16[4,640]{1,0:T(4,128)(2,1)S(1)}, bf16[4,640]{1,0:T(4,128)(2,1)}, u32[]{:S(2)}) copy-start(bf16[4,640]{1,0:T(4,128)(2,1)} %param.19) | copy-start | bytes 15364
  6.5 8.8 %copy-start.10 = (f32[2,256,10]{1,0,2:T(2,128)S(1)}, f32[2,256,10]{1,0,2:T(2,128)}, u32[]{:S(2)}) copy-start(f32[2,256,10]{1,0,2:T(2,128)} %param.17) | copy-start | bytes 61444
  6.5 92.6 %all-gather.6.cloned.1.call-start = ((), (), s32[]{:S(2)}) async-start(), calls=%async_computation.1 | async-start | bytes 1638400 | tf_op jit(solution)/shard_map/all_gather | solution.py:32
  10.9 14.4 %copy-start.12 = (s32[2,256]{1,0:T(2,128)S(1)}, s32[2,256]{1,0:T(2,128)}, u32[]{:S(2)}) copy-start(s32[2,256]{1,0:T(2,128)} %param.18) | copy-start | bytes 6148
  12.8 15.5 %collective-permute-start = (bf16[2,3,897]{1,2,0:T(8,128)(2,1)}, bf16[2,3,897]{1,2,0:T(8,128)(2,1)}, u32[]{:S(2)}, u32[]{:S(2)}) collective-permute-start(bf16[2,3,897]{1,2,0:T(8,128)(2,1)} %pad_maximum_fusion.1), channel_id=1, source_target_pairs={{0,8},{8,16},{16,24},{24,32},{32,40},{40,48},{48,56},{56,64},{64,7... | collective-permute-start | bytes 32300 | tf_op jit(solution)/shard_map/ppermute | solution.py:18
  36.4 0.7 copy-start.5
  42.3 3.8 %copy-start.4 = (bf16[2,256,640]{1,2,0:T(8,128)(2,1)S(1)}, bf16[2,256,640]{1,2,0:T(8,128)(2,1)}, u32[]{:S(2)}) copy-start(bf16[2,256,640]{1,2,0:T(8,128)(2,1)} %copy.162) | copy-start | bytes 1966084
  43.0 5.4 %copy-start.9 = (f32[2,256,10]{1,2,0:T(8,128)S(1)}, f32[2,256,10]{1,2,0:T(8,128)}, u32[]{:S(2)}) copy-start(f32[2,256,10]{1,2,0:T(8,128)} %copy.177) | copy-start | bytes 61444
  43.0 5.4 %copy-start.28 = (f32[2,10]{1,0:T(2,128)S(1)}, f32[2,10]{1,0:T(2,128)}, u32[]{:S(2)}) copy-start(f32[2,10]{1,0:T(2,128)} %multiply_bitcast_fusion) | copy-start | bytes 244
  48.3 4.7 %copy-start.7 = (bf16[2,256,640]{1,2,0:T(8,128)(2,1)}, bf16[2,256,640]{1,2,0:T(8,128)(2,1)S(1)}, u32[]{:S(2)}) copy-start(bf16[2,256,640]{1,2,0:T(8,128)(2,1)S(1)} %multiply_convert_fusion.3) | copy-start | bytes 1966084
  53.1 14.7 %copy-start.3 = (bf16[4,10,64,128]{3,2,1,0:T(8,128)(2,1)}, bf16[4,10,64,128]{3,2,1,0:T(8,128)(2,1)S(1)}, u32[]{:S(2)}) copy-start(bf16[4,10,64,128]{3,2,1,0:T(8,128)(2,1)S(1)} %all-gather.1) | copy-start | bytes 1966084
  67.8 0.6 copy-start.24
  67.8 0.6 copy-start.26
  67.8 33.6 %copy-start.17 = (bf16[2,10]{1,0:T(2,128)(2,1)}, bf16[2,10]{1,0:T(2,128)(2,1)S(1)}, u32[]{:S(2)}) copy-start(bf16[2,10]{1,0:T(2,128)(2,1)S(1)} %get-tuple-element.11) | copy-start | bytes 124
  67.8 33.6 %copy-start.19 = (bf16[2,10]{1,0:T(2,128)(2,1)}, bf16[2,10]{1,0:T(2,128)(2,1)S(1)}, u32[]{:S(2)}) copy-start(bf16[2,10]{1,0:T(2,128)(2,1)S(1)} %get-tuple-element.12) | copy-start | bytes 124
  67.8 33.6 %copy-start.21 = (bf16[2,10]{1,0:T(2,128)(2,1)}, bf16[2,10]{1,0:T(2,128)(2,1)S(1)}, u32[]{:S(2)}) copy-start(bf16[2,10]{1,0:T(2,128)(2,1)S(1)} %get-tuple-element.13) | copy-start | bytes 124
  69.2 79.3 %all-gather.8.cloned.1.call-start = ((), (), s32[]{:S(2)}) async-start(), calls=%async_computation.2 | async-start | bytes 2949120 | tf_op jit(solution)/shard_map/all_gather | solution.py:32
  101.4 26.6 %copy-start.13 = (pred[2,256]{1,0:T(4,128)(4,1)S(1)}, pred[2,256]{1,0:T(4,128)(4,1)}, u32[]{:S(2)}) copy-start(pred[2,256]{1,0:T(4,128)(4,1)} %get-tuple-element.36) | copy-start | bytes 1540
  101.4 26.6 %copy-start.14 = (pred[2,256]{1,0:T(4,128)(4,1)S(1)}, pred[2,256]{1,0:T(4,128)(4,1)}, u32[]{:S(2)}) copy-start(pred[2,256]{1,0:T(4,128)(4,1)} %get-tuple-element.37) | copy-start | bytes 1540
  101.4 26.6 %copy-start.15 = (pred[2,256]{1,0:T(4,128)(4,1)S(1)}, pred[2,256]{1,0:T(4,128)(4,1)}, u32[]{:S(2)}) copy-start(pred[2,256]{1,0:T(4,128)(4,1)} %get-tuple-element.38) | copy-start | bytes 1540
  101.4 127.6 %reduce-scatter.4.cloned.1.call-start = ((), (), s32[]{:S(2)}) async-start(), calls=%async_computation.3 | async-start | bytes 2949120
  103.8 4.5 %copy-start.6 = (f32[2,256,10]{2,0,1:T(2,128)S(1)}, f32[2,256,10]{2,0,1:T(2,128)}, u32[]{:S(2)}) copy-start(f32[2,256,10]{2,0,1:T(2,128)} %copy-done.5) | copy-start | bytes 61444
  130.7 17.9 %copy-start.8 = (f32[2,256,10]{1,2,0:T(8,128)S(1)}, f32[2,256,10]{1,2,0:T(8,128)}, u32[]{:S(2)}) copy-start(f32[2,256,10]{1,2,0:T(8,128)} %copy.174) | copy-start | bytes 61444
  130.7 17.9 %copy-start.18 = (bf16[2,10]{1,0:T(2,128)(2,1)S(1)}, bf16[2,10]{1,0:T(2,128)(2,1)}, u32[]{:S(2)}) copy-start(bf16[2,10]{1,0:T(2,128)(2,1)} %copy-done.17) | copy-start | bytes 124
  130.7 17.9 %copy-start.20 = (bf16[2,10]{1,0:T(2,128)(2,1)S(1)}, bf16[2,10]{1,0:T(2,128)(2,1)}, u32[]{:S(2)}) copy-start(bf16[2,10]{1,0:T(2,128)(2,1)} %copy-done.19) | copy-start | bytes 124
  130.7 17.9 %copy-start.22 = (bf16[2,10]{1,0:T(2,128)(2,1)S(1)}, bf16[2,10]{1,0:T(2,128)(2,1)}, u32[]{:S(2)}) copy-start(bf16[2,10]{1,0:T(2,128)(2,1)} %copy-done.21) | copy-start | bytes 124
  130.7 17.9 %copy-start.23 = (bf16[2,10]{1,0:T(2,128)(2,1)S(1)}, bf16[2,10]{1,0:T(2,128)(2,1)}, u32[]{:S(2)}) copy-start(bf16[2,10]{1,0:T(2,128)(2,1)} %get-tuple-element.44) | copy-start | bytes 124
  130.7 17.9 %copy-start.25 = (bf16[2,10]{1,0:T(2,128)(2,1)S(1)}, bf16[2,10]{1,0:T(2,128)(2,1)}, u32[]{:S(2)}) copy-start(bf16[2,10]{1,0:T(2,128)(2,1)} %copy-done.24) | copy-start | bytes 124
  130.7 17.9 %copy-start.27 = (bf16[2,10]{1,0:T(2,128)(2,1)S(1)}, bf16[2,10]{1,0:T(2,128)(2,1)}, u32[]{:S(2)}) copy-start(bf16[2,10]{1,0:T(2,128)(2,1)} %copy-done.26) | copy-start | bytes 124
  130.7 17.9 %copy-start.29 = (bf16[2,10]{1,0:T(2,128)(2,1)S(1)}, bf16[2,10]{1,0:T(2,128)(2,1)}, u32[]{:S(2)}) copy-start(bf16[2,10]{1,0:T(2,128)(2,1)} %get-tuple-element.9) | copy-start | bytes 124
  130.7 17.9 %copy-start.30 = (bf16[2,10]{1,0:T(2,128)(2,1)S(1)}, bf16[2,10]{1,0:T(2,128)(2,1)}, u32[]{:S(2)}) copy-start(bf16[2,10]{1,0:T(2,128)(2,1)} %get-tuple-element.10) | copy-start | bytes 124
  148.6 5.5 %copy-start.1 = (bf16[2,256,640]{1,2,0:T(8,128)(2,1)S(1)}, bf16[2,256,640]{1,2,0:T(8,128)(2,1)}, u32[]{:S(2)}) copy-start(bf16[2,256,640]{1,2,0:T(8,128)(2,1)} %copy.178) | copy-start | bytes 1966084
  153.0 1.1 copy-start.2
  154.1 17.7 %copy-start.16 = (f32[640]{0:T(1024)S(1)}, f32[640]{0:T(1024)}, u32[]{:S(2)}) copy-start(f32[640]{0:T(1024)} %param.24) | copy-start | bytes 7684
Sparse Core Ops, SparseCore 0:
  69.4 29.7 all-gather.5
  101.5 47.0 all-gather.7
  186.1 42.7 reduce-scatter.3
where the time goes:
time: 241 us; the launch traced here: 239 us
  waiting for transfers between devices  86.8 us (36%)
  blocking collectives  51.5 us (21%)
  local copies, waits for them, and re-layouts  38.6 us (16%)
  other arithmetic  31.5 us (13%)
  matrix products  15.4 us (6%)
  between operations  13.4 us (6%)
    all_gather x2, waiting for transfers between devices, carried_in(): pieces = jax.tree.map(lambda part: lax.all_gather(part, axis), total)  43.8 us
    unnamed x4, waiting for transfers between devices  43 us
    all_gather x4, blocking collectives, carried_in(): pieces = jax.tree.map(lambda part: lax.all_gather(part, axis), total)  34.3 us
    psum x1, blocking collectives, shards(): squares = lax.psum(jnp.sum(gated * gated, axis=2), 'mp')  17.2 us
    unnamed x68, local copies, waits for them, and re-layouts  14 us
  transfers between devices with their start and end apart: 4, of which 3 were waited for; matrix products, arithmetic and copies ran while one was open for 12% of the time, Pallas kernels for 0%

commit v1 on v0

v1 whole, which is shorter than its diff:
```python
import functools

import jax
import jax.numpy as jnp
from jax import lax
from jax.experimental import pallas as pl
from jax.experimental.pallas import tpu as pltpu
from jax.sharding import Mesh
from jax.sharding import PartitionSpec as P

SPLIT = (8, 4, 2)
SEQ = ("sz", "sx", "sc")
INNER = 5120
EPSILON = 1e-05
BATCH = 2
LENGTH = 256
HALF = 128
HALO = 8
TAPS = 4
HEADDIM = 64
DSTATE = 128
REACH = 8192 // LENGTH
F32 = jnp.float32
BF16 = jnp.bfloat16
LANES = (((1,), (1,)), ((), ()))
ROWS = (((0,), (0,)), ((), ()))


def dot(a, b, dims):
    return lax.dot_general(a, b, dims, preferred_element_type=F32)


def split_two(value):
    high = value.astype(BF16)
    return high, (value - high.astype(F32)).astype(BF16)


def silu(value):
    return value / (1.0 + jnp.exp(-value))


class Plan:
    def __init__(self, split, members, channels, width):
        self.planes, self.xs, self.cores = split
        self.ring = self.xs * self.cores
        self.members = members
        self.channels = channels
        self.heads = channels // HEADDIM
        self.pairs = self.heads // 2
        self.conv = channels + 2 * DSTATE
        self.shard = channels // self.ring
        self.groups = self.shard // 16
        self.gate_rows = 8 if self.groups <= 8 else 16
        self.packet = self.shard + 2 * self.gate_rows
        self.reach = min(-(-REACH // self.ring), self.planes - 1)
        self.width = width
        self.out = width // members
        self.far = members // 2


def spread(rows, plan):
    return jnp.concatenate(
        [jnp.broadcast_to(rows[q : q + 1], (16, DSTATE)) for q in range(plan.groups)], axis=0
    )


def pair_columns(cols, first, lane):
    a = jnp.broadcast_to(cols[:, first : first + 1], (cols.shape[0], 128))
    b = jnp.broadcast_to(cols[:, first + 1 : first + 2], (cols.shape[0], 128))
    return jnp.where(lane < HEADDIM, a, b)


def layer_kernel(
    plan,
    x_hbm,
    z_hbm,
    b_hbm,
    c_hbm,
    dt_hbm,
    doc_hbm,
    cx_hbm,
    cb_hbm,
    cc_hbm,
    bias_ref,
    rate_ref,
    gain_ref,
    w_hbm,
    out_ref,
    xbc,
    halo,
    docs_ref,
    doc_halo,
    dt_ref,
    taps,
    z_ref,
    w_ref,
    wt,
    conv,
    masks,
    xw,
    y,
    scores,
    zg,
    gated,
    fsend,
    arecv,
    pref,
    qpref,
    tsend,
    brecv,
    hsend,
    hstate,
    part,
    up_recv,
    dn_recv,
    ssend,
    srecv,
    load_sem,
    halo_send,
    halo_recv,
    a_send,
    a_recv,
    b_send,
    b_recv,
    c_send,
    c_recv,
    s_send,
    s_recv,
    up_send,
    up_got,
    dn_send,
    dn_got,
):
    ch, nh, ring, members = plan.channels, plan.heads, plan.ring, plan.members
    iz, ix, ic = lax.axis_index("sz"), lax.axis_index("sx"), lax.axis_index("sc")
    me = lax.axis_index("mp")
    rank = ix * plan.cores + ic
    place = iz * ring + rank
    blocks = plan.planes * ring

    def in_plane(r):
        return {"sx": r // plan.cores, "sc": r % plan.cores}

    def in_line(j):
        return {"sz": j // ring, "sx": (j % ring) // plan.cores, "sc": j % plan.cores}

    after = in_line(lax.rem(place + 1, blocks))
    prior = in_line(lax.rem(place + blocks - 1, blocks))
    up = {"mp": lax.rem(me + 1, members)}
    down = {"mp": lax.rem(me + members - 1, members)}

    barrier = pltpu.get_barrier_semaphore()
    count = 0
    greet = [after, prior]
    greet += [in_plane(lax.rem(rank + k, ring)) for k in range(1, ring)]
    for k in range(1, plan.reach + 1):
        greet.append({"sz": lax.rem(iz + k, plan.planes)})
        greet.append({"sz": lax.rem(iz + plan.planes - k, plan.planes)})
    greet += [{"mp": lax.rem(me + k, members)} for k in range(1, members)]
    for peer in greet:
        pl.semaphore_signal(barrier, inc=1, device_id=peer, device_id_type=pl.DeviceIdType.MESH)
        count += 1

    loads = []

    def load(src, dst):
        copy = pltpu.make_async_copy(src, dst, load_sem.at[len(loads)])
        copy.start()
        loads.append(copy)
        return copy

    got_dt = load(dt_hbm, dt_ref)
    got_docs = load(doc_hbm, docs_ref)
    got_taps = [
        load(cx_hbm, taps.at[:, pl.ds(0, ch)]),
        load(cb_hbm, taps.at[:, pl.ds(ch, DSTATE)]),
        load(cc_hbm, taps.at[:, pl.ds(ch + DSTATE, DSTATE)]),
    ]
    got_rows = []
    for m in range(BATCH):
        got_rows.append(
            [
                load(x_hbm.at[m], xbc.at[m, :, pl.ds(0, ch)]),
                load(b_hbm.at[m], xbc.at[m, :, pl.ds(ch, DSTATE)]),
                load(c_hbm.at[m], xbc.at[m, :, pl.ds(ch + DSTATE, DSTATE)]),
            ]
        )
    got_z = load(z_hbm, z_ref)
    got_w = load(w_hbm, w_ref)

    lane = lax.broadcasted_iota(jnp.int32, (LENGTH, 128), 1)

    got_docs.wait()
    got_dt.wait()
    docs = docs_ref[...].astype(F32)
    head_row = lax.broadcasted_iota(jnp.int32, (16, LENGTH), 0)
    bias = jnp.zeros((16, LENGTH), F32)
    rate = jnp.zeros((16, LENGTH), F32)
    for h in range(nh):
        bias = jnp.where(head_row == h, bias_ref[h], bias)
        rate = jnp.where(head_row == h, rate_ref[h], rate)
    step_rows, log_parts = [], []
    for m in range(BATCH):
        raw = dt_ref[:, m, :]
        if nh < 16:
            raw = jnp.concatenate([raw, jnp.zeros((16 - nh, LENGTH), F32)], axis=0)
        shifted = raw + bias
        step = jnp.maximum(shifted, 0.0) + jnp.log1p(jnp.exp(-jnp.abs(shifted)))
        step_rows.append(step)
        log_parts.append(-(step * rate))
    log_step = jnp.concatenate(log_parts, axis=0)
    hi = log_step.astype(BF16)
    rest = log_step - hi.astype(F32)
    mid = rest.astype(BF16)
    low = (rest - mid.astype(F32)).astype(BF16)
    before = lax.broadcasted_iota(jnp.int32, (LENGTH, LENGTH), 0) <= lax.broadcasted_iota(
        jnp.int32, (LENGTH, LENGTH), 1
    )
    upper = jnp.where(before, 1.0, 0.0).astype(BF16)
    sums = dot(jnp.concatenate([low, mid, hi], axis=0), upper, (((1,), (0,)), ((), ())))
    span = BATCH * 16
    log_cum = sums[0:span] + sums[span : 2 * span] + sums[2 * span : 3 * span]
    log_rows = [log_cum[m * 16 : (m + 1) * 16] for m in range(BATCH)]
    row_mats = list(log_rows)
    ends = []
    for m in range(BATCH):
        end = log_rows[m][:, LENGTH - 1 : LENGTH]
        ends.append(end)
        keep = jnp.where(docs[m : m + 1] == docs[m : m + 1, LENGTH - 1 : LENGTH], 1.0, 0.0)
        row_mats.append(jnp.exp(jnp.minimum(end - log_rows[m], 0.0)) * step_rows[m] * keep)
    for m in range(BATCH):
        row_mats.append(jnp.exp(log_rows[m]))
    marks = []
    for m in range(BATCH):
        own = docs[m : m + 1]
        marks.append(own)
        for k in range(1, TAPS):
            marks.append(jnp.where(pltpu.roll(own, k, 1) == own, 1.0, 0.0))
    row_mats.append(jnp.concatenate(marks + [jnp.zeros((32 - len(marks), LENGTH), F32)], axis=0))
    cols = jnp.concatenate(row_mats, axis=0).T
    log_col, weight_col, entry_col, mark_col = 0, span, 2 * span, 3 * span

    for copy in got_taps:
        copy.wait()
    tap = taps[...].astype(F32)
    tiles = plan.conv // 128
    for m in range(BATCH):
        for k in range(1, TAPS):
            at = mark_col + m * TAPS + k
            masks[m, k - 1] = jnp.broadcast_to(cols[:, at : at + 1], (LENGTH, 128))
    for m in range(BATCH):
        for copy in got_rows[m]:
            copy.wait()
        for j in range(tiles):
            at = slice(j * 128, (j + 1) * 128)
            rows = xbc[m, :, at].astype(F32)
            total = rows * tap[TAPS - 1 : TAPS, at]
            for k in range(1, TAPS):
                weight = tap[TAPS - 1 - k : TAPS - k, at]
                total = total + (pltpu.roll(rows, k, 0) * weight) * masks[m, k - 1]
            total = silu(total)
            conv[m, :, at] = total.astype(BF16)
            if j < plan.pairs:
                scale = pair_columns(cols, weight_col + m * 16 + 2 * j, lane)
                xw[m, :, at] = (total.astype(BF16).astype(F32) * scale).astype(BF16)

    pl.semaphore_wait(barrier, count)

    halos = []
    for m in range(BATCH):
        halos.append(
            pltpu.make_async_remote_copy(
                src_ref=xbc.at[m, pl.ds(LENGTH - HALO, HALO)],
                dst_ref=halo.at[m],
                send_sem=halo_send.at[m],
                recv_sem=halo_recv.at[m],
                device_id=after,
                device_id_type=pl.DeviceIdType.MESH,
            )
        )
    halos.append(
        pltpu.make_async_remote_copy(
            src_ref=docs_ref.at[:, pl.ds(LENGTH - 128, 128)],
            dst_ref=doc_halo,
            send_sem=halo_send.at[BATCH],
            recv_sem=halo_recv.at[BATCH],
            device_id=after,
            device_id_type=pl.DeviceIdType.MESH,
        )
    )
    for copy in (halos[BATCH], *halos[:BATCH]):
        copy.start()

    got_w.wait()
    for j in range(plan.width // 128):
        wt[j * 128 : (j + 1) * 128, :] = w_ref[:, j * 128 : (j + 1) * 128].T
    got_z.wait()
    for m in range(BATCH):
        for j in range(plan.pairs):
            at = slice(j * 128, (j + 1) * 128)
            zg[m, :, at] = silu(z_ref[m, :, at].astype(F32))

    halos[BATCH].wait()
    doc_before = jnp.where(place == 0, -1.0, doc_halo[...].astype(F32))
    edge_marks = []
    joined = jnp.concatenate([doc_before, docs[:, 0:128]], axis=1)
    for k in range(1, TAPS):
        edge_marks.append(jnp.where(pltpu.roll(joined, k, 1) == joined, 1.0, 0.0))
    edge_rows = jnp.concatenate(
        edge_marks + [jnp.zeros((16 - BATCH * (TAPS - 1), LENGTH), F32)], axis=0
    )[:, 128:256]
    edge_rows = jnp.concatenate([edge_rows, jnp.zeros((112, 128), F32)], axis=0)
    edge_cols = edge_rows.T[0:HALO]

    def exchange(m, source, target, peers_send, peers_recv):
        copies = []
        for k in range(1, ring):
            to = lax.rem(rank + k, ring)
            copies.append(
                pltpu.make_async_remote_copy(
                    src_ref=source.at[m, to],
                    dst_ref=target(to),
                    send_sem=peers_send.at[m, k],
                    recv_sem=peers_recv.at[m, k],
                    device_id=in_plane(to),
                    device_id_type=pl.DeviceIdType.MESH,
                )
            )
        return copies

    group_row = lax.broadcasted_iota(jnp.int32, (ring * plan.gate_rows, 16), 0)
    group_head = lax.broadcasted_iota(jnp.int32, (ring * plan.gate_rows, 16), 1)
    bits = plan.gate_rows.bit_length() - 1
    shard_of, group_of = group_row >> bits, group_row & (plan.gate_rows - 1)
    picks = (((shard_of * plan.groups + group_of) >> 2) == group_head) & (group_of < plan.groups)
    pick = jnp.where(picks, 1.0, 0.0).astype(BF16)
    a_copies = []
    for m in range(BATCH):
        halos[m].wait()
        for j in range(tiles):
            at = slice(j * 128, (j + 1) * 128)
            lead = halo[m, :, at].astype(F32)
            own = xbc[m, 0:HALO, at].astype(F32)
            both = jnp.concatenate([lead, own], axis=0)
            total = own * tap[TAPS - 1 : TAPS, at]
            for k in range(1, TAPS):
                weight = tap[TAPS - 1 - k : TAPS - k, at]
                same = edge_cols[:, (k - 1) * BATCH + m : (k - 1) * BATCH + m + 1]
                total = total + (pltpu.roll(both, k, 0)[HALO : 2 * HALO] * weight) * same
            total = silu(total)
            conv[m, 0:HALO, at] = total.astype(BF16)
            if j < plan.pairs:
                scale = pair_columns(cols[0:HALO], weight_col + m * 16 + 2 * j, lane[0:HALO])
                xw[m, 0:HALO, at] = (total.astype(BF16).astype(F32) * scale).astype(BF16)
        state = dot(xw[m], conv[m, :, ch : ch + DSTATE], ROWS).astype(BF16)
        carried_end = docs[m : m + 1, LENGTH - 1 : LENGTH] == doc_before[m : m + 1, 127:128]
        gate = jnp.broadcast_to(jnp.exp(ends[m]) * jnp.where(carried_end, 1.0, 0.0), (16, DSTATE))
        gate_hi, gate_lo = split_two(gate)
        plain = (((1,), (0,)), ((), ()))
        hi_rows = dot(pick, gate_hi, plain).astype(BF16)
        lo_rows = dot(pick, gate_lo, plain).astype(BF16)
        for r in range(ring):
            fsend[m, r, 0 : plan.shard] = state[r * plan.shard : (r + 1) * plan.shard]
            at = slice(r * plan.gate_rows, (r + 1) * plan.gate_rows)
            fsend[m, r, plan.shard : plan.packet] = jnp.concatenate(
                [hi_rows[at], lo_rows[at]], axis=0
            )
        copies = exchange(m, fsend, lambda to, m=m: arecv.at[m, rank], a_send, a_recv)
        for copy in copies:
            copy.start()
        a_copies.append(copies)
        arecv[m, pl.ds(rank, 1)] = fsend[m, pl.ds(rank, 1)]

    def scores_of(m):
        t_pos = lax.broadcasted_iota(jnp.int32, (LENGTH, LENGTH), 0)
        s_pos = lax.broadcasted_iota(jnp.int32, (LENGTH, LENGTH), 1)
        doc_t = cols[:, mark_col + m * TAPS : mark_col + m * TAPS + 1]
        keep = (s_pos <= t_pos) & (doc_t == docs[m : m + 1])
        full = dot(conv[m, :, ch + DSTATE : ch + 2 * DSTATE], conv[m, :, ch : ch + DSTATE], LANES)
        scores[m] = jnp.where(keep, full, 0.0)

    def inner_of(m):
        low_lane = lane < HEADDIM
        for j in range(plan.pairs):
            at = slice(j * 128, (j + 1) * 128)
            xs = conv[m, :, at]
            xs_a = jnp.where(low_lane, xs, jnp.zeros_like(xs))
            xs_b = jnp.where(low_lane, jnp.zeros_like(xs), xs)
            for half in range(2):
                t0, s1 = half * HALF, (half + 1) * HALF
                base = scores[m, t0 : t0 + HALF, 0:s1]
                mixes = []
                for h in (2 * j, 2 * j + 1):
                    t_log = cols[t0 : t0 + HALF, log_col + m * 16 + h : log_col + m * 16 + h + 1]
                    s_log = log_rows[m][h : h + 1, 0:s1]
                    decay = jnp.exp(jnp.minimum(t_log - s_log, 0.0))
                    mixes.append((base * step_rows[m][h : h + 1, 0:s1] * decay).astype(BF16))
                y[m, t0 : t0 + HALF, at] = dot(
                    jnp.concatenate(mixes, axis=1),
                    jnp.concatenate([xs_a[0:s1], xs_b[0:s1]], axis=0),
                    (((1,), (0,)), ((), ())),
                )

    b_copies = []
    for m in range(BATCH):
        scores_of(m)
    for m in range(BATCH):
        for copy in a_copies[m]:
            copy.wait_recv()
        total = jnp.zeros((plan.shard, DSTATE), F32)
        product = jnp.ones((plan.gate_rows, DSTATE), F32)
        for d in range(ring):
            pref[m, d] = total
            qpref[m, d] = product
            packet = arecv[m, d].astype(F32)
            gates = (
                packet[plan.shard : plan.shard + plan.gate_rows]
                + packet[plan.shard + plan.gate_rows :]
            )
            total = spread(gates, plan) * total + packet[0 : plan.shard]
            product = product * gates
        tsend[m, 0 : plan.shard] = total.astype(BF16)
        hi_rows, lo_rows = split_two(product)
        tsend[m, plan.shard : plan.packet] = jnp.concatenate([hi_rows, lo_rows], axis=0)
        copies = []
        for k in range(1, plan.reach + 1):
            copy = pltpu.make_async_remote_copy(
                src_ref=tsend.at[m],
                dst_ref=brecv.at[m, k - 1],
                send_sem=b_send.at[m, k - 1],
                recv_sem=b_recv.at[m, k - 1],
                device_id={"sz": lax.rem(iz + k, plan.planes)},
                device_id_type=pl.DeviceIdType.MESH,
            )
            copy.start()
            copies.append(copy)
        b_copies.append(copies)
        if m == 0:
            inner_of(0)

    c_copies = []
    for m in range(BATCH):
        for copy in b_copies[m]:
            copy.wait_recv()
        incoming = jnp.zeros((plan.shard, DSTATE), F32)
        for k in range(plan.reach, 0, -1):
            packet = brecv[m, k - 1].astype(F32)
            gates = (
                packet[plan.shard : plan.shard + plan.gate_rows]
                + packet[plan.shard + plan.gate_rows :]
            )
            fresh = jnp.where(iz >= k, packet[0 : plan.shard], 0.0)
            incoming = spread(gates, plan) * incoming + fresh
            incoming = jnp.where(iz >= k, incoming, 0.0)
        for d in range(ring):
            entering = pref[m, d] + spread(qpref[m, d], plan) * incoming
            hsend[m, d] = entering.astype(BF16)
        home = pl.ds(pl.multiple_of(rank * plan.shard, 16), plan.shard)
        copies = exchange(m, hsend, lambda to, m=m: hstate.at[m, home], c_send, c_recv)
        for copy in copies:
            copy.start()
        c_copies.append(copies)
        hstate[m, home] = hsend[m, rank]
        if m == 0:
            inner_of(1)

    def arrow(chunk, step, upward):
        if upward:
            owner = lax.rem(me + plan.far - step, members)
            first, buffer, send, got, to = 0, up_recv, up_send, up_got, up
        else:
            owner = lax.rem(me + members - plan.far + step, members)
            first, buffer, send, got, to = plan.out // 2, dn_recv, dn_send, dn_got, down
        rows = pl.ds(first, plan.out // 2) if step == 0 else pl.ds(0, plan.out)
        return pltpu.make_async_remote_copy(
            src_ref=part.at[chunk, owner, rows],
            dst_ref=buffer.at[chunk, step, rows],
            send_sem=send.at[chunk, step],
            recv_sem=got.at[chunk, step],
            device_id=to,
            device_id_type=pl.DeviceIdType.MESH,
        )

    arrows = {}
    s_copies = []
    gain = gain_ref[...]
    for m in range(BATCH):
        for copy in c_copies[m]:
            copy.wait_recv()
        carried = cols[:, mark_col + m * TAPS : mark_col + m * TAPS + 1] == doc_before[m : m + 1, 127:128]
        squares = jnp.zeros((LENGTH, 128), F32)
        outer = dot(conv[m, :, ch + DSTATE : ch + 2 * DSTATE], hstate[m], LANES)
        for j in range(plan.pairs):
            at = slice(j * 128, (j + 1) * 128)
            entry = pair_columns(cols, entry_col + m * 16 + 2 * j, lane)
            entry = jnp.where(carried, entry, 0.0)
            mixed = (y[m, :, at] + entry * outer[:, at]) * zg[m, :, at]
            squares = squares + mixed * mixed
            gated[m, :, at] = (mixed * gain[:, at]).astype(BF16)
        square_hi, square_lo = split_two(squares)
        ones = jnp.ones((8, 128), BF16)
        square_rows = dot(ones, square_hi, LANES) + dot(ones, square_lo, LANES)
        ssend[m] = square_rows[0:1]

        def project(owner, m=m):
            rows = pl.ds(pl.multiple_of(owner * plan.out, 16), plan.out)
            tile = dot(wt[rows, :], gated[m], LANES).astype(BF16)
            part[2 * m, owner] = tile[:, 0:HALF]
            part[2 * m + 1, owner] = tile[:, HALF:LENGTH]

        project(lax.rem(me + plan.far, members))
        for chunk in (2 * m, 2 * m + 1):
            for upward in (True, False):
                arrows[chunk, 0, upward] = arrow(chunk, 0, upward)
                arrows[chunk, 0, upward].start()
        for k in range(1, members):
            copy = pltpu.make_async_remote_copy(
                src_ref=ssend.at[m],
                dst_ref=srecv.at[m, k],
                send_sem=s_send.at[m, k],
                recv_sem=s_recv.at[m, k],
                device_id={"mp": lax.rem(me + k, members)},
                device_id_type=pl.DeviceIdType.MESH,
            )
            copy.start()
            s_copies.append(copy)
        for step in range(1, plan.far):
            project(lax.rem(me + plan.far - step, members))
            project(lax.rem(me + members - plan.far + step, members))
        project(me)

    half = plan.out // 2
    chunks = range(2 * BATCH)
    for step in range(1, plan.far):
        for chunk in chunks:
            for upward in (True, False):
                arrows[chunk, step - 1, upward].wait_recv()
                buffer = up_recv if upward else dn_recv
                if upward:
                    owner = lax.rem(me + plan.far - step, members)
                else:
                    owner = lax.rem(me + members - plan.far + step, members)
                if step == 1:
                    rows = slice(0, half) if upward else slice(half, plan.out)
                else:
                    rows = slice(0, plan.out)
                total = part[chunk, owner, rows].astype(F32) + buffer[chunk, step - 1, rows].astype(F32)
                part[chunk, owner, rows] = total.astype(BF16)
                arrows[chunk, step, upward] = arrow(chunk, step, upward)
                arrows[chunk, step, upward].start()

    for copy in s_copies:
        copy.wait_recv()
    last = plan.far - 1
    for m in range(BATCH):
        square = ssend[m]
        for k in range(1, members):
            square = square + srecv[m, k]
        scale = lax.rsqrt(square / INNER + EPSILON)
        for side in range(2):
            chunk = 2 * m + side
            total = part[chunk, me].astype(F32)
            if last == 0:
                arrows[chunk, last, True].wait_recv()
                arrows[chunk, last, False].wait_recv()
                total = total + jnp.concatenate(
                    [up_recv[chunk, 0, 0:half], dn_recv[chunk, 0, half : plan.out]], axis=0
                ).astype(F32)
            else:
                for upward in (True, False):
                    arrows[chunk, last, upward].wait_recv()
                    buffer = up_recv if upward else dn_recv
                    total = total + buffer[chunk, last].astype(F32)
            at = slice(side * HALF, (side + 1) * HALF)
            out_ref[m, :, at] = (total * scale[:, at]).astype(BF16)

    for copy in halos:
        pass
    for group in (*a_copies, *b_copies, *c_copies, s_copies, list(arrows.values())):
        for copy in group:
            copy.wait_send()


def shards(
    plan,
    x_inner,
    z_gate,
    b_input,
    c_input,
    dt_raw,
    doc_ids,
    conv_x,
    conv_b,
    conv_c,
    dt_bias,
    decay_rate,
    norm_gain,
    w_out,
):
    hbm = pl.BlockSpec(memory_space=pltpu.HBM)
    smem = pl.BlockSpec(memory_space=pltpu.SMEM)
    vmem = pl.BlockSpec(memory_space=pltpu.VMEM)
    ch, ring, members = plan.channels, plan.ring, plan.members
    chunks = 2 * BATCH
    dma = pltpu.SemaphoreType.DMA
    reach = max(plan.reach, 1)
    scratch = [
        pltpu.VMEM((BATCH, LENGTH, plan.conv), BF16),
        pltpu.VMEM((BATCH, HALO, plan.conv), BF16),
        pltpu.VMEM((BATCH, LENGTH), jnp.int32),
        pltpu.VMEM((BATCH, 128), jnp.int32),
        pltpu.VMEM((plan.heads, BATCH, LENGTH), F32),
        pltpu.VMEM((TAPS, plan.conv), BF16),
        pltpu.VMEM((BATCH, LENGTH, ch), BF16),
        pltpu.VMEM((ch, plan.width), BF16),
        pltpu.VMEM((plan.width, ch), BF16),
        pltpu.VMEM((BATCH, LENGTH, plan.conv), BF16),
        pltpu.VMEM((BATCH, TAPS - 1, LENGTH, 128), F32),
        pltpu.VMEM((BATCH, LENGTH, ch), BF16),
        pltpu.VMEM((BATCH, LENGTH, ch), F32),
        pltpu.VMEM((BATCH, LENGTH, LENGTH), F32),
        pltpu.VMEM((BATCH, LENGTH, ch), F32),
        pltpu.VMEM((BATCH, LENGTH, ch), BF16),
        pltpu.VMEM((BATCH, ring, plan.packet, DSTATE), BF16),
        pltpu.VMEM((BATCH, ring, plan.packet, DSTATE), BF16),
        pltpu.VMEM((BATCH, ring, plan.shard, DSTATE), F32),
        pltpu.VMEM((BATCH, ring, plan.gate_rows, DSTATE), F32),
        pltpu.VMEM((BATCH, plan.packet, DSTATE), BF16),
        pltpu.VMEM((BATCH, reach, plan.packet, DSTATE), BF16),
        pltpu.VMEM((BATCH, ring, plan.shard, DSTATE), BF16),
        pltpu.VMEM((BATCH, ch, DSTATE), BF16),
        pltpu.VMEM((chunks, members, plan.out, HALF), BF16),
        pltpu.VMEM((chunks, plan.far, plan.out, HALF), BF16),
        pltpu.VMEM((chunks, plan.far, plan.out, HALF), BF16),
        pltpu.VMEM((BATCH, 1, LENGTH), F32),
        pltpu.VMEM((BATCH, members, 1, LENGTH), F32),
        dma((13,)),
        dma((BATCH + 1,)),
        dma((BATCH + 1,)),
        dma((BATCH, ring)),
        dma((BATCH, ring)),
        dma((BATCH, reach)),
        dma((BATCH, reach)),
        dma((BATCH, ring)),
        dma((BATCH, ring)),
        dma((BATCH, members)),
        dma((BATCH, members)),
        dma((chunks, plan.far)),
        dma((chunks, plan.far)),
        dma((chunks, plan.far)),
        dma((chunks, plan.far)),
    ]
    out = pl.pallas_call(
        functools.partial(layer_kernel, plan),
        name="mixer_layer",
        out_shape=jax.ShapeDtypeStruct((BATCH, plan.out, LENGTH), BF16),
        in_specs=[hbm] * 9 + [smem, smem, vmem, hbm],
        out_specs=vmem,
        scratch_shapes=scratch,
        compiler_params=pltpu.CompilerParams(
            collective_id=0, has_side_effects=True, vmem_limit_bytes=60 * 1024 * 1024
        ),
    )(
        x_inner,
        z_gate,
        b_input,
        c_input,
        jnp.transpose(dt_raw, (2, 0, 1)),
        doc_ids,
        conv_x,
        conv_b,
        conv_c,
        dt_bias,
        decay_rate,
        norm_gain.reshape(1, ch),
        w_out,
    )
    return jnp.transpose(out, (0, 2, 1))


def solution(mesh):
    members = mesh.shape["mp"]
    line = Mesh(mesh.devices.reshape(*SPLIT, members), (*SEQ, "mp"))

    def layer(*arrays):
        channels = arrays[0].shape[2] // members
        plan = Plan(SPLIT, members, channels, arrays[12].shape[1])
        placed = (
            P(None, SEQ, "mp"),
            P(None, SEQ, "mp"),
            P(None, SEQ, None),
            P(None, SEQ, None),
            P(None, SEQ, "mp"),
            P(None, SEQ),
            P(None, "mp"),
            P(),
            P(),
            P("mp"),
            P("mp"),
            P("mp"),
            P("mp", None),
        )
        return jax.shard_map(
            functools.partial(shards, plan),
            mesh=line,
            in_specs=placed,
            out_specs=P(None, SEQ, "mp"),
            check_vma=False,
        )(*arrays)

    return layer
```

time: 241 us -> 72.6 us (0.30)
  the two profiles are of different devices: /device:TPU:2 before, /device:TPU:1 now
where the time goes in v1:
time: 72.6 us; the launch traced here: 72.4 us
  Pallas kernels  69.4 us (96%)
  local copies, waits for them, and re-layouts  2.98 us (4%)
    pallas_call x1, Pallas kernels, shards(): pl.pallas_call(functools.partial(layer_kernel, plan), name='mixer_layer',...  69.4 us
    unnamed x1, local copies, waits for them, and re-layouts  1.72 us

profile of v1, /device:TPU:1, one launch (start us, length us, event | category | flops | bytes accessed | tf_op | source)
XLA Modules:
  0.0 72.4 jit_solution(3912175165738434537)
XLA Ops:
  0.0 1.3 %reshape.3.gain_ref = f32[1,640]{1,0:T(1,128)} reshape(f32[640]{0:T(1024)} %param.24) | data formatting | bytes 5120 | tf_op jit(solution)/shard_map/reshape | solution.py:675
  1.3 69.4 %mixer_layer.1 = bf16[2,320,256]{2,1,0:T(8,128)(2,1)} custom-call(bf16[2,256,640]{2,1,0:T(8,128)(2,1)} %x_hbm.1, bf16[2,256,640]{2,1,0:T(8,128)(2,1)} %z_hbm.1, bf16[2,256,128]{2,1,0:T(8,128)(2,1)} %b_hbm.1, bf16[2,256,128]{2,1,0:T(8,128)(2,1)} %c_hbm.1, f32[10,2,256]{2,1,0:T(2,128)} %bitcast.3, s32[2,256]{1,0:T(2,128)} %doc_hbm.1, bf16[4,640]{1,0:T(4,128)(2,1)} %cx_hbm.1, ...), custom_call_target="tpu_custom_call" | custom-call | tf_op jit(solution)/shard_map/mixer_layer/pallas_call | solution.py:653
  70.7 1.7 %copy.15 = bf16[2,256,320]{1,2,0:T(8,128)(2,1)} copy(bf16[2,256,320]{1,2,0:T(8,128)(2,1)} %bitcast.2) | data formatting | bytes 655360

commit v2 on v1

--- a/solution.py
+++ b/solution.py
@@ -144,22 +144,29 @@
     def in_line(j):
         return {"sz": j // ring, "sx": (j % ring) // plan.cores, "sc": j % plan.cores}
 
-    after = in_line(lax.rem(place + 1, blocks))
-    prior = in_line(lax.rem(place + blocks - 1, blocks))
+    after, prior = in_line(place + 1), in_line(place - 1)
     up = {"mp": lax.rem(me + 1, members)}
     down = {"mp": lax.rem(me + members - 1, members)}
 
+    has_next, has_prior = place + 1 < blocks, place > 0
+
+    def one(flag):
+        return jnp.where(flag, 1, 0)
+
     barrier = pltpu.get_barrier_semaphore()
-    count = 0
-    greet = [after, prior]
-    greet += [in_plane(lax.rem(rank + k, ring)) for k in range(1, ring)]
+
+    def greet(peer):
+        pl.semaphore_signal(barrier, inc=1, device_id=peer, device_id_type=pl.DeviceIdType.MESH)
+
+    for k in range(1, ring):
+        greet(in_plane(lax.rem(rank + k, ring)))
+    for k in range(1, members):
+        greet({"mp": lax.rem(me + k, members)})
+    pl.when(has_prior)(lambda: greet(prior))
+    count = ring - 1 + members - 1 + one(has_next)
     for k in range(1, plan.reach + 1):
-        greet.append({"sz": lax.rem(iz + k, plan.planes)})
-        greet.append({"sz": lax.rem(iz + plan.planes - k, plan.planes)})
-    greet += [{"mp": lax.rem(me + k, members)} for k in range(1, members)]
-    for peer in greet:
-        pl.semaphore_signal(barrier, inc=1, device_id=peer, device_id_type=pl.DeviceIdType.MESH)
-        count += 1
+        pl.when(iz >= k)(lambda k=k: greet({"sz": iz - k}))
+        count = count + one(iz + k < plan.planes)
 
     loads = []
 
@@ -168,6 +175,17 @@
         copy.start()
         loads.append(copy)
         return copy
+
+    done = []
+
+    def need(copy):
+        if not any(copy is other for other in done):
+            copy.wait()
+            done.append(copy)
+
+    def got_waits():
+        for copy in loads:
+            need(copy)
 
     got_dt = load(dt_hbm, dt_ref)
     got_docs = load(doc_hbm, docs_ref)
@@ -190,8 +208,8 @@
 
     lane = lax.broadcasted_iota(jnp.int32, (LENGTH, 128), 1)
 
-    got_docs.wait()
-    got_dt.wait()
+    need(got_docs)
+    need(got_dt)
     docs = docs_ref[...].astype(F32)
     head_row = lax.broadcasted_iota(jnp.int32, (16, LENGTH), 0)
     bias = jnp.zeros((16, LENGTH), F32)
@@ -241,16 +259,16 @@
     log_col, weight_col, entry_col, mark_col = 0, span, 2 * span, 3 * span
 
     for copy in got_taps:
-        copy.wait()
+        need(copy)
     tap = taps[...].astype(F32)
     tiles = plan.conv // 128
     for m in range(BATCH):
         for k in range(1, TAPS):
             at = mark_col + m * TAPS + k
             masks[m, k - 1] = jnp.broadcast_to(cols[:, at : at + 1], (LENGTH, 128))
-    for m in range(BATCH):
+    def convolve(m):
         for copy in got_rows[m]:
-            copy.wait()
+            need(copy)
         for j in range(tiles):
             at = slice(j * 128, (j + 1) * 128)
             rows = xbc[m, :, at].astype(F32)
@@ -264,6 +282,9 @@
                 scale = pair_columns(cols, weight_col + m * 16 + 2 * j, lane)
                 xw[m, :, at] = (total.astype(BF16).astype(F32) * scale).astype(BF16)
 
+    convolve(0)
+    for copy in got_rows[1]:
+        need(copy)
     pl.semaphore_wait(barrier, count)
 
     halos = []
@@ -288,20 +309,26 @@
             device_id_type=pl.DeviceIdType.MESH,
         )
     )
-    for copy in (halos[BATCH], *halos[:BATCH]):
-        copy.start()
-
-    got_w.wait()
-    for j in range(plan.width // 128):
-        wt[j * 128 : (j + 1) * 128, :] = w_ref[:, j * 128 : (j + 1) * 128].T
-    got_z.wait()
-    for m in range(BATCH):
+    def send_halo():
+        for copy in (halos[BATCH], *halos[:BATCH]):
+            copy.start()
+
+    pl.when(has_next)(send_halo)
+    convolve(1)
+
+    def turn_weights():
+        need(got_w)
+        for j in range(plan.width // 128):
+            wt[j * 128 : (j + 1) * 128, :] = w_ref[:, j * 128 : (j + 1) * 128].T
+
+    def gate_inputs(m):
+        need(got_z)
         for j in range(plan.pairs):
             at = slice(j * 128, (j + 1) * 128)
             zg[m, :, at] = silu(z_ref[m, :, at].astype(F32))
 
-    halos[BATCH].wait()
-    doc_before = jnp.where(place == 0, -1.0, doc_halo[...].astype(F32))
+    pl.when(has_prior)(halos[BATCH].wait_recv)
+    doc_before = jnp.where(has_prior, doc_halo[...].astype(F32), -1.0)
     edge_marks = []
     joined = jnp.concatenate([doc_before, docs[:, 0:128]], axis=1)
     for k in range(1, TAPS):
@@ -336,10 +363,10 @@
     pick = jnp.where(picks, 1.0, 0.0).astype(BF16)
     a_copies = []
     for m in range(BATCH):
-        halos[m].wait()
+        pl.when(has_prior)(halos[m].wait_recv)
         for j in range(tiles):
             at = slice(j * 128, (j + 1) * 128)
-            lead = halo[m, :, at].astype(F32)
+            lead = jnp.where(has_prior, halo[m, :, at].astype(F32), 0.0)
             own = xbc[m, 0:HALO, at].astype(F32)
             both = jnp.concatenate([lead, own], axis=0)
             total = own * tap[TAPS - 1 : TAPS, at]
@@ -401,9 +428,11 @@
                     (((1,), (0,)), ((), ())),
                 )
 
+    gate_inputs(0)
+    gate_inputs(1)
+    scores_of(0)
+    scores_of(1)
     b_copies = []
-    for m in range(BATCH):
-        scores_of(m)
     for m in range(BATCH):
         for copy in a_copies[m]:
             copy.wait_recv()
@@ -429,19 +458,20 @@
                 dst_ref=brecv.at[m, k - 1],
                 send_sem=b_send.at[m, k - 1],
                 recv_sem=b_recv.at[m, k - 1],
-                device_id={"sz": lax.rem(iz + k, plan.planes)},
+                device_id={"sz": iz + k},
                 device_id_type=pl.DeviceIdType.MESH,
             )
-            copy.start()
+            pl.when(iz + k < plan.planes)(copy.start)
             copies.append(copy)
         b_copies.append(copies)
-        if m == 0:
-            inner_of(0)
-
+
+    turn_weights()
+    inner_of(0)
+    inner_of(1)
     c_copies = []
     for m in range(BATCH):
-        for copy in b_copies[m]:
-            copy.wait_recv()
+        for k in range(plan.reach, 0, -1):
+            pl.when(iz >= k)(b_copies[m][k - 1].wait_recv)
         incoming = jnp.zeros((plan.shard, DSTATE), F32)
         for k in range(plan.reach, 0, -1):
             packet = brecv[m, k - 1].astype(F32)
@@ -461,8 +491,6 @@
             copy.start()
         c_copies.append(copies)
         hstate[m, home] = hsend[m, rank]
-        if m == 0:
-            inner_of(1)
 
     def arrow(chunk, step, upward):
         if upward:
@@ -483,7 +511,7 @@
 
     arrows = {}
     s_copies = []
-    gain = gain_ref[...]
+    gain = gain_ref[...].reshape(1, ch)
     for m in range(BATCH):
         for copy in c_copies[m]:
             copy.wait_recv()
@@ -574,11 +602,17 @@
             at = slice(side * HALF, (side + 1) * HALF)
             out_ref[m, :, at] = (total * scale[:, at]).astype(BF16)
 
-    for copy in halos:
-        pass
-    for group in (*a_copies, *b_copies, *c_copies, s_copies, list(arrows.values())):
+    def sent():
+        for copy in halos:
+            copy.wait_send()
+
+    pl.when(has_next)(sent)
+    for group in (*a_copies, *c_copies, s_copies, list(arrows.values())):
         for copy in group:
             copy.wait_send()
+    for m in range(BATCH):
+        for k in range(1, plan.reach + 1):
+            pl.when(iz + k < plan.planes)(b_copies[m][k - 1].wait_send)
 
 
 def shards(
@@ -672,7 +706,7 @@
         conv_c,
         dt_bias,
         decay_rate,
-        norm_gain.reshape(1, ch),
+        norm_gain,
         w_out,
     )
     return jnp.transpose(out, (0, 2, 1))

time: 72.6 us -> 64.2 us (0.88)
  the two profiles are of different devices: /device:TPU:1 before, /device:TPU:384 now
where the time goes in v2:
time: 64.2 us; the launch traced here: 64.1 us
  Pallas kernels  62.3 us (97%)
  local copies, waits for them, and re-layouts  1.72 us (3%)
    pallas_call x1, Pallas kernels, shards(): pl.pallas_call(functools.partial(layer_kernel, plan), name='mixer_layer',...  62.3 us
    unnamed x1, local copies, waits for them, and re-layouts  1.72 us

profile of v2, /device:TPU:384, one launch (start us, length us, event | category | flops | bytes accessed | tf_op | source)
XLA Modules:
  0.0 64.1 jit_solution(5855526520386368638)
XLA Ops:
  0.0 62.3 %mixer_layer.1 = bf16[2,320,256]{2,1,0:T(8,128)(2,1)} custom-call(bf16[2,256,640]{2,1,0:T(8,128)(2,1)} %x_hbm.1, bf16[2,256,640]{2,1,0:T(8,128)(2,1)} %z_hbm.1, bf16[2,256,128]{2,1,0:T(8,128)(2,1)} %b_hbm.1, bf16[2,256,128]{2,1,0:T(8,128)(2,1)} %c_hbm.1, f32[10,2,256]{2,1,0:T(2,128)} %bitcast.3, s32[2,256]{1,0:T(2,128)} %doc_hbm.1, bf16[4,640]{1,0:T(4,128)(2,1)} %cx_hbm.1, ...), custom_call_target="tpu_custom_call" | custom-call | tf_op jit(solution)/shard_map/mixer_layer/pallas_call | solution.py:687
  62.3 1.7 %copy.15 = bf16[2,256,320]{1,2,0:T(8,128)(2,1)} copy(bf16[2,256,320]{1,2,0:T(8,128)(2,1)} %bitcast.2) | data formatting | bytes 655360

commit v3 on v2

--- a/solution.py
+++ b/solution.py
@@ -53,6 +53,7 @@
         self.gate_rows = 8 if self.groups <= 8 else 16
         self.packet = self.shard + 2 * self.gate_rows
         self.reach = min(-(-REACH // self.ring), self.planes - 1)
+        assert self.reach <= 4
         self.width = width
         self.out = width // members
         self.far = members // 2
@@ -130,6 +131,7 @@
     up_got,
     dn_send,
     dn_got,
+    word,
 ):
     ch, nh, ring, members = plan.channels, plan.heads, plan.ring, plan.members
     iz, ix, ic = lax.axis_index("sz"), lax.axis_index("sx"), lax.axis_index("sc")
@@ -164,9 +166,21 @@
         greet({"mp": lax.rem(me + k, members)})
     pl.when(has_prior)(lambda: greet(prior))
     count = ring - 1 + members - 1 + one(has_next)
-    for k in range(1, plan.reach + 1):
-        pl.when(iz >= k)(lambda k=k: greet({"sz": iz - k}))
-        count = count + one(iz + k < plan.planes)
+    above, below = {"sz": iz + 1}, {"sz": iz - 1}
+    has_above, has_below = iz + 1 < plan.planes, iz > 0
+    pl.when(has_below)(lambda: greet(below))
+    pl.when(has_above)(lambda: greet(above))
+    count = count + one(has_above) + one(has_below)
+
+    def pass_word(k):
+        pl.when(has_below & (iz + k - 1 < plan.planes))(
+            lambda: pl.semaphore_signal(
+                word.at[k], inc=1, device_id=below, device_id_type=pl.DeviceIdType.MESH
+            )
+        )
+
+    def hear_word(k):
+        pl.when(iz + k < plan.planes)(lambda: pl.semaphore_wait(word.at[k], 1))
 
     loads = []
 
@@ -286,6 +300,8 @@
     for copy in got_rows[1]:
         need(copy)
     pl.semaphore_wait(barrier, count)
+    if plan.reach >= 2:
+        pass_word(2)
 
     halos = []
     for m in range(BATCH):
@@ -430,7 +446,15 @@
 
     gate_inputs(0)
     gate_inputs(1)
+    if plan.reach >= 2:
+        hear_word(2)
+    if plan.reach >= 3:
+        pass_word(3)
     scores_of(0)
+    if plan.reach >= 3:
+        hear_word(3)
+    if plan.reach >= 4:
+        pass_word(4)
     scores_of(1)
     b_copies = []
     for m in range(BATCH):
@@ -452,6 +476,8 @@
         hi_rows, lo_rows = split_two(product)
         tsend[m, plan.shard : plan.packet] = jnp.concatenate([hi_rows, lo_rows], axis=0)
         copies = []
+        if m == 0 and plan.reach >= 4:
+            hear_word(4)
         for k in range(1, plan.reach + 1):
             copy = pltpu.make_async_remote_copy(
                 src_ref=tsend.at[m],
@@ -683,11 +709,12 @@
         dma((chunks, plan.far)),
         dma((chunks, plan.far)),
         dma((chunks, plan.far)),
+        pltpu.SemaphoreType.REGULAR((5,)),
     ]
     out = pl.pallas_call(
         functools.partial(layer_kernel, plan),
         name="mixer_layer",
-        out_shape=jax.ShapeDtypeStruct((BATCH, plan.out, LENGTH), BF16),
+        out_shape=pltpu.VMEM((BATCH, plan.out, LENGTH), BF16),
         in_specs=[hbm] * 9 + [smem, smem, vmem, hbm],
         out_specs=vmem,
         scratch_shapes=scratch,

time: 64.2 us -> 59.6 us (0.928)
  Pallas kernels: 62.3 us -> 58.7 us
  local copies, waits for them, and re-layouts: 1.72 us -> 0.73 us
    pallas_call x1, Pallas kernels: 62.3 us -> 58.7 us  [shards(): pl.pallas_call(functools.partial(layer_kernel, plan), name='mixer_layer',...]
    unnamed x1, local copies, waits for them, and re-layouts: 1.72 us -> 0.73 us
where the time goes in v3:
time: 59.6 us; the launch traced here: 59.4 us
  Pallas kernels  58.7 us (98%)
  local copies, waits for them, and re-layouts  0.73 us (1%)
    pallas_call x1, Pallas kernels, shards(): pl.pallas_call(functools.partial(layer_kernel, plan), name='mixer_layer',...  58.7 us

profile of v3, /device:TPU:384, one launch (start us, length us, event | category | flops | bytes accessed | tf_op | source)
XLA Modules:
  0.0 59.4 jit_solution(15830781269884524879)
XLA Ops:
  0.0 58.7 %mixer_layer.1 = bf16[2,320,256]{2,1,0:T(8,128)(2,1)S(1)} custom-call(bf16[2,256,640]{2,1,0:T(8,128)(2,1)} %x_hbm.1, bf16[2,256,640]{2,1,0:T(8,128)(2,1)} %z_hbm.1, bf16[2,256,128]{2,1,0:T(8,128)(2,1)} %b_hbm.1, bf16[2,256,128]{2,1,0:T(8,128)(2,1)} %c_hbm.1, f32[10,2,256]{2,1,0:T(2,128)} %bitcast.3, s32[2,256]{1,0:T(2,128)} %doc_hbm.1, ...), custom_call_target="tpu_custom_call" | custom-call | tf_op jit(solution)/shard_map/mixer_layer/pallas_call | solution.py:714
  58.7 0.7 %copy.15 = bf16[2,256,320]{1,2,0:T(8,128)(2,1)} copy(bf16[2,256,320]{1,2,0:T(8,128)(2,1)S(1)} %bitcast.2) | data formatting | bytes 655360

commit v4 on v3

--- a/solution.py
+++ b/solution.py
@@ -444,6 +444,15 @@
                     (((1,), (0,)), ((), ())),
                 )
 
+    def gate_both(m):
+        carried = cols[:, mark_col + m * TAPS : mark_col + m * TAPS + 1] == doc_before[m : m + 1, 127:128]
+        for j in range(plan.pairs):
+            at = slice(j * 128, (j + 1) * 128)
+            opened = zg[m, :, at]
+            y[m, :, at] = y[m, :, at] * opened
+            entry = pair_columns(cols, entry_col + m * 16 + 2 * j, lane)
+            zg[m, :, at] = jnp.where(carried, entry, 0.0) * opened
+
     gate_inputs(0)
     gate_inputs(1)
     if plan.reach >= 2:
@@ -493,7 +502,9 @@
 
     turn_weights()
     inner_of(0)
+    gate_both(0)
     inner_of(1)
+    gate_both(1)
     c_copies = []
     for m in range(BATCH):
         for k in range(plan.reach, 0, -1):
@@ -538,35 +549,32 @@
     arrows = {}
     s_copies = []
     gain = gain_ref[...].reshape(1, ch)
-    for m in range(BATCH):
+
+    def project(m, owner):
+        rows = pl.ds(pl.multiple_of(owner * plan.out, 16), plan.out)
+        tile = dot(wt[rows, :], gated[m], LANES).astype(BF16)
+        part[2 * m, owner] = tile[:, 0:HALF]
+        part[2 * m + 1, owner] = tile[:, HALF:LENGTH]
+
+    def carry(m):
         for copy in c_copies[m]:
             copy.wait_recv()
-        carried = cols[:, mark_col + m * TAPS : mark_col + m * TAPS + 1] == doc_before[m : m + 1, 127:128]
         squares = jnp.zeros((LENGTH, 128), F32)
         outer = dot(conv[m, :, ch + DSTATE : ch + 2 * DSTATE], hstate[m], LANES)
         for j in range(plan.pairs):
             at = slice(j * 128, (j + 1) * 128)
-            entry = pair_columns(cols, entry_col + m * 16 + 2 * j, lane)
-            entry = jnp.where(carried, entry, 0.0)
-            mixed = (y[m, :, at] + entry * outer[:, at]) * zg[m, :, at]
+            mixed = y[m, :, at] + zg[m, :, at] * outer[:, at]
             squares = squares + mixed * mixed
             gated[m, :, at] = (mixed * gain[:, at]).astype(BF16)
+        project(m, lax.rem(me + plan.far, members))
+        for chunk in (2 * m, 2 * m + 1):
+            for upward in (True, False):
+                arrows[chunk, 0, upward] = arrow(chunk, 0, upward)
+                arrows[chunk, 0, upward].start()
         square_hi, square_lo = split_two(squares)
         ones = jnp.ones((8, 128), BF16)
         square_rows = dot(ones, square_hi, LANES) + dot(ones, square_lo, LANES)
         ssend[m] = square_rows[0:1]
-
-        def project(owner, m=m):
-            rows = pl.ds(pl.multiple_of(owner * plan.out, 16), plan.out)
-            tile = dot(wt[rows, :], gated[m], LANES).astype(BF16)
-            part[2 * m, owner] = tile[:, 0:HALF]
-            part[2 * m + 1, owner] = tile[:, HALF:LENGTH]
-
-        project(lax.rem(me + plan.far, members))
-        for chunk in (2 * m, 2 * m + 1):
-            for upward in (True, False):
-                arrows[chunk, 0, upward] = arrow(chunk, 0, upward)
-                arrows[chunk, 0, upward].start()
         for k in range(1, members):
             copy = pltpu.make_async_remote_copy(
                 src_ref=ssend.at[m],
@@ -578,22 +586,21 @@
             )
             copy.start()
             s_copies.append(copy)
-        for step in range(1, plan.far):
-            project(lax.rem(me + plan.far - step, members))
-            project(lax.rem(me + members - plan.far + step, members))
-        project(me)
 
     half = plan.out // 2
-    chunks = range(2 * BATCH)
-    for step in range(1, plan.far):
-        for chunk in chunks:
+
+    def ring_step(m, step):
+        owners = {
+            True: lax.rem(me + plan.far - step, members),
+            False: lax.rem(me + members - plan.far + step, members),
+        }
+        for upward in (True, False):
+            project(m, owners[upward])
+        for chunk in (2 * m, 2 * m + 1):
             for upward in (True, False):
                 arrows[chunk, step - 1, upward].wait_recv()
                 buffer = up_recv if upward else dn_recv
-                if upward:
-                    owner = lax.rem(me + plan.far - step, members)
-                else:
-                    owner = lax.rem(me + members - plan.far + step, members)
+                owner = owners[upward]
                 if step == 1:
                     rows = slice(0, half) if upward else slice(half, plan.out)
                 else:
@@ -602,6 +609,17 @@
                 part[chunk, owner, rows] = total.astype(BF16)
                 arrows[chunk, step, upward] = arrow(chunk, step, upward)
                 arrows[chunk, step, upward].start()
+
+    carry(0)
+    if plan.far > 1:
+        ring_step(0, 1)
+    carry(1)
+    for step in range(1, plan.far):
+        if step > 1:
+            ring_step(0, step)
+        ring_step(1, step)
+    for m in range(BATCH):
+        project(m, me)
 
     for copy in s_copies:
         copy.wait_recv()

time: 59.6 us -> 59.5 us (level)
  no operation moved by 1% of the time
where the time goes in v4:
time: 59.5 us; the launch traced here: 59.4 us
  Pallas kernels  58.6 us (98%)
  local copies, waits for them, and re-layouts  0.73 us (1%)
    pallas_call x1, Pallas kernels, shards(): pl.pallas_call(functools.partial(layer_kernel, plan), name='mixer_layer',...  58.6 us

profile of v4, /device:TPU:384, one launch (start us, length us, event | category | flops | bytes accessed | tf_op | source)
XLA Modules:
  0.0 59.4 jit_solution(1700575287035094716)
XLA Ops:
  0.0 58.6 %mixer_layer.1 = bf16[2,320,256]{2,1,0:T(8,128)(2,1)S(1)} custom-call(bf16[2,256,640]{2,1,0:T(8,128)(2,1)} %x_hbm.1, bf16[2,256,640]{2,1,0:T(8,128)(2,1)} %z_hbm.1, bf16[2,256,128]{2,1,0:T(8,128)(2,1)} %b_hbm.1, bf16[2,256,128]{2,1,0:T(8,128)(2,1)} %c_hbm.1, f32[10,2,256]{2,1,0:T(2,128)} %bitcast.3, s32[2,256]{1,0:T(2,128)} %doc_hbm.1, ...), custom_call_target="tpu_custom_call" | custom-call | tf_op jit(solution)/shard_map/mixer_layer/pallas_call | solution.py:732
  58.6 0.7 %copy.15 = bf16[2,256,320]{1,2,0:T(8,128)(2,1)} copy(bf16[2,256,320]{1,2,0:T(8,128)(2,1)S(1)} %bitcast.2) | data formatting | bytes 655360

commit v5 on v4

--- a/solution.py
+++ b/solution.py
@@ -50,10 +50,9 @@
         self.conv = channels + 2 * DSTATE
         self.shard = channels // self.ring
         self.groups = self.shard // 16
-        self.gate_rows = 8 if self.groups <= 8 else 16
+        self.gate_rows = max(8, 1 << (self.groups - 1).bit_length())
         self.packet = self.shard + 2 * self.gate_rows
-        self.reach = min(-(-REACH // self.ring), self.planes - 1)
-        assert self.reach <= 4
+        assert REACH <= 4 * self.ring or self.planes <= 5
         self.width = width
         self.out = width // members
         self.far = members // 2
@@ -108,6 +107,9 @@
     pref,
     qpref,
     tsend,
+    usend,
+    ptot,
+    qtot,
     brecv,
     hsend,
     hstate,
@@ -172,15 +174,10 @@
     pl.when(has_above)(lambda: greet(above))
     count = count + one(has_above) + one(has_below)
 
-    def pass_word(k):
-        pl.when(has_below & (iz + k - 1 < plan.planes))(
-            lambda: pl.semaphore_signal(
-                word.at[k], inc=1, device_id=below, device_id_type=pl.DeviceIdType.MESH
-            )
+    def tell_below(at):
+        pl.semaphore_signal(
+            word.at[at], inc=1, device_id=below, device_id_type=pl.DeviceIdType.MESH
         )
-
-    def hear_word(k):
-        pl.when(iz + k < plan.planes)(lambda: pl.semaphore_wait(word.at[k], 1))
 
     loads = []
 
@@ -220,88 +217,11 @@
     got_z = load(z_hbm, z_ref)
     got_w = load(w_hbm, w_ref)
 
-    lane = lax.broadcasted_iota(jnp.int32, (LENGTH, 128), 1)
-
     need(got_docs)
-    need(got_dt)
-    docs = docs_ref[...].astype(F32)
-    head_row = lax.broadcasted_iota(jnp.int32, (16, LENGTH), 0)
-    bias = jnp.zeros((16, LENGTH), F32)
-    rate = jnp.zeros((16, LENGTH), F32)
-    for h in range(nh):
-        bias = jnp.where(head_row == h, bias_ref[h], bias)
-        rate = jnp.where(head_row == h, rate_ref[h], rate)
-    step_rows, log_parts = [], []
-    for m in range(BATCH):
-        raw = dt_ref[:, m, :]
-        if nh < 16:
-            raw = jnp.concatenate([raw, jnp.zeros((16 - nh, LENGTH), F32)], axis=0)
-        shifted = raw + bias
-        step = jnp.maximum(shifted, 0.0) + jnp.log1p(jnp.exp(-jnp.abs(shifted)))
-        step_rows.append(step)
-        log_parts.append(-(step * rate))
-    log_step = jnp.concatenate(log_parts, axis=0)
-    hi = log_step.astype(BF16)
-    rest = log_step - hi.astype(F32)
-    mid = rest.astype(BF16)
-    low = (rest - mid.astype(F32)).astype(BF16)
-    before = lax.broadcasted_iota(jnp.int32, (LENGTH, LENGTH), 0) <= lax.broadcasted_iota(
-        jnp.int32, (LENGTH, LENGTH), 1
-    )
-    upper = jnp.where(before, 1.0, 0.0).astype(BF16)
-    sums = dot(jnp.concatenate([low, mid, hi], axis=0), upper, (((1,), (0,)), ((), ())))
-    span = BATCH * 16
-    log_cum = sums[0:span] + sums[span : 2 * span] + sums[2 * span : 3 * span]
-    log_rows = [log_cum[m * 16 : (m + 1) * 16] for m in range(BATCH)]
-    row_mats = list(log_rows)
-    ends = []
-    for m in range(BATCH):
-        end = log_rows[m][:, LENGTH - 1 : LENGTH]
-        ends.append(end)
-        keep = jnp.where(docs[m : m + 1] == docs[m : m + 1, LENGTH - 1 : LENGTH], 1.0, 0.0)
-        row_mats.append(jnp.exp(jnp.minimum(end - log_rows[m], 0.0)) * step_rows[m] * keep)
-    for m in range(BATCH):
-        row_mats.append(jnp.exp(log_rows[m]))
-    marks = []
-    for m in range(BATCH):
-        own = docs[m : m + 1]
-        marks.append(own)
-        for k in range(1, TAPS):
-            marks.append(jnp.where(pltpu.roll(own, k, 1) == own, 1.0, 0.0))
-    row_mats.append(jnp.concatenate(marks + [jnp.zeros((32 - len(marks), LENGTH), F32)], axis=0))
-    cols = jnp.concatenate(row_mats, axis=0).T
-    log_col, weight_col, entry_col, mark_col = 0, span, 2 * span, 3 * span
-
-    for copy in got_taps:
-        need(copy)
-    tap = taps[...].astype(F32)
-    tiles = plan.conv // 128
-    for m in range(BATCH):
-        for k in range(1, TAPS):
-            at = mark_col + m * TAPS + k
-            masks[m, k - 1] = jnp.broadcast_to(cols[:, at : at + 1], (LENGTH, 128))
-    def convolve(m):
-        for copy in got_rows[m]:
-            need(copy)
-        for j in range(tiles):
-            at = slice(j * 128, (j + 1) * 128)
-            rows = xbc[m, :, at].astype(F32)
-            total = rows * tap[TAPS - 1 : TAPS, at]
-            for k in range(1, TAPS):
-                weight = tap[TAPS - 1 - k : TAPS - k, at]
-                total = total + (pltpu.roll(rows, k, 0) * weight) * masks[m, k - 1]
-            total = silu(total)
-            conv[m, :, at] = total.astype(BF16)
-            if j < plan.pairs:
-                scale = pair_columns(cols, weight_col + m * 16 + 2 * j, lane)
-                xw[m, :, at] = (total.astype(BF16).astype(F32) * scale).astype(BF16)
-
-    convolve(0)
-    for copy in got_rows[1]:
+    for copy in (*got_rows[0], *got_rows[1]):
         need(copy)
     pl.semaphore_wait(barrier, count)
-    if plan.reach >= 2:
-        pass_word(2)
+    pl.when(has_below & has_above)(lambda: tell_below(0))
 
     halos = []
     for m in range(BATCH):
@@ -330,7 +250,80 @@
             copy.start()
 
     pl.when(has_next)(send_halo)
-    convolve(1)
+
+    lane = lax.broadcasted_iota(jnp.int32, (LENGTH, 128), 1)
+
+    docs = docs_ref[...].astype(F32)
+    marks = []
+    for m in range(BATCH):
+        own = docs[m : m + 1]
+        marks.append(own)
+        for k in range(1, TAPS):
+            marks.append(jnp.where(pltpu.roll(own, k, 1) == own, 1.0, 0.0))
+    mark_cols = jnp.concatenate(marks, axis=0).T
+    for m in range(BATCH):
+        for k in range(1, TAPS):
+            at = m * TAPS + k
+            masks[m, k - 1] = jnp.broadcast_to(mark_cols[:, at : at + 1], (LENGTH, 128))
+    need(got_dt)
+    head_row = lax.broadcasted_iota(jnp.int32, (16, LENGTH), 0)
+    bias = jnp.zeros((16, LENGTH), F32)
+    rate = jnp.zeros((16, LENGTH), F32)
+    for h in range(nh):
+        bias = jnp.where(head_row == h, bias_ref[h], bias)
+        rate = jnp.where(head_row == h, rate_ref[h], rate)
+    step_rows, log_parts = [], []
+    for m in range(BATCH):
+        raw = dt_ref[:, m, :]
+        if nh < 16:
+            raw = jnp.concatenate([raw, jnp.zeros((16 - nh, LENGTH), F32)], axis=0)
+        shifted = raw + bias
+        step = jnp.maximum(shifted, 0.0) + jnp.log1p(jnp.exp(-jnp.abs(shifted)))
+        step_rows.append(step)
+        log_parts.append(-(step * rate))
+    log_step = jnp.concatenate(log_parts, axis=0)
+    hi = log_step.astype(BF16)
+    rest = log_step - hi.astype(F32)
+    mid = rest.astype(BF16)
+    low = (rest - mid.astype(F32)).astype(BF16)
+    before = lax.broadcasted_iota(jnp.int32, (LENGTH, LENGTH), 0) <= lax.broadcasted_iota(
+        jnp.int32, (LENGTH, LENGTH), 1
+    )
+    upper = jnp.where(before, 1.0, 0.0).astype(BF16)
+    sums = dot(jnp.concatenate([low, mid, hi], axis=0), upper, (((1,), (0,)), ((), ())))
+    span = BATCH * 16
+    log_cum = sums[0:span] + sums[span : 2 * span] + sums[2 * span : 3 * span]
+    log_rows = [log_cum[m * 16 : (m + 1) * 16] for m in range(BATCH)]
+    row_mats = list(log_rows)
+    ends = []
+    for m in range(BATCH):
+        end = log_rows[m][:, LENGTH - 1 : LENGTH]
+        ends.append(end)
+        keep = jnp.where(docs[m : m + 1] == docs[m : m + 1, LENGTH - 1 : LENGTH], 1.0, 0.0)
+        row_mats.append(jnp.exp(jnp.minimum(end - log_rows[m], 0.0)) * step_rows[m] * keep)
+    for m in range(BATCH):
+        row_mats.append(jnp.exp(log_rows[m]))
+    row_mats.append(jnp.zeros((128 - 3 * span, LENGTH), F32))
+    cols = jnp.concatenate(row_mats, axis=0).T
+    log_col, weight_col, entry_col = 0, span, 2 * span
+
+    for copy in got_taps:
+        need(copy)
+    tap = taps[...].astype(F32)
+    tiles = plan.conv // 128
+    def convolve(m):
+        for j in range(tiles):
+            at = slice(j * 128, (j + 1) * 128)
+            rows = xbc[m, :, at].astype(F32)
+            total = rows * tap[TAPS - 1 : TAPS, at]
+            for k in range(1, TAPS):
+                weight = tap[TAPS - 1 - k : TAPS - k, at]
+                total = total + (pltpu.roll(rows, k, 0) * weight) * masks[m, k - 1]
+            total = silu(total)
+            conv[m, :, at] = total.astype(BF16)
+            if j < plan.pairs:
+                scale = pair_columns(cols, weight_col + m * 16 + 2 * j, lane)
+                xw[m, :, at] = (total.astype(BF16).astype(F32) * scale).astype(BF16)
 
     def turn_weights():
         need(got_w)
@@ -343,6 +336,7 @@
             at = slice(j * 128, (j + 1) * 128)
             zg[m, :, at] = silu(z_ref[m, :, at].astype(F32))
 
+    convolve(0)
     pl.when(has_prior)(halos[BATCH].wait_recv)
     doc_before = jnp.where(has_prior, doc_halo[...].astype(F32), -1.0)
     edge_marks = []
@@ -379,6 +373,8 @@
     pick = jnp.where(picks, 1.0, 0.0).astype(BF16)
     a_copies = []
     for m in range(BATCH):
+        if m > 0:
+            convolve(m)
         pl.when(has_prior)(halos[m].wait_recv)
         for j in range(tiles):
             at = slice(j * 128, (j + 1) * 128)
@@ -417,7 +413,7 @@
     def scores_of(m):
         t_pos = lax.broadcasted_iota(jnp.int32, (LENGTH, LENGTH), 0)
         s_pos = lax.broadcasted_iota(jnp.int32, (LENGTH, LENGTH), 1)
-        doc_t = cols[:, mark_col + m * TAPS : mark_col + m * TAPS + 1]
+        doc_t = mark_cols[:, m * TAPS : m * TAPS + 1]
         keep = (s_pos <= t_pos) & (doc_t == docs[m : m + 1])
         full = dot(conv[m, :, ch + DSTATE : ch + 2 * DSTATE], conv[m, :, ch : ch + DSTATE], LANES)
         scores[m] = jnp.where(keep, full, 0.0)
@@ -445,7 +441,7 @@
                 )
 
     def gate_both(m):
-        carried = cols[:, mark_col + m * TAPS : mark_col + m * TAPS + 1] == doc_before[m : m + 1, 127:128]
+        carried = mark_cols[:, m * TAPS : m * TAPS + 1] == doc_before[m : m + 1, 127:128]
         for j in range(plan.pairs):
             at = slice(j * 128, (j + 1) * 128)
             opened = zg[m, :, at]
@@ -453,20 +449,35 @@
             entry = pair_columns(cols, entry_col + m * 16 + 2 * j, lane)
             zg[m, :, at] = jnp.where(carried, entry, 0.0) * opened
 
-    gate_inputs(0)
-    gate_inputs(1)
-    if plan.reach >= 2:
-        hear_word(2)
-    if plan.reach >= 3:
-        pass_word(3)
-    scores_of(0)
-    if plan.reach >= 3:
-        hear_word(3)
-    if plan.reach >= 4:
-        pass_word(4)
-    scores_of(1)
-    b_copies = []
-    for m in range(BATCH):
+    def unpack(packet):
+        packet = packet.astype(F32)
+        split = plan.shard + plan.gate_rows
+        return packet[0 : plan.shard], packet[plan.shard : split] + packet[split:]
+
+    def pack(ref, m, total, product):
+        ref[m, 0 : plan.shard] = total.astype(BF16)
+        hi_rows, lo_rows = split_two(product)
+        ref[m, plan.shard : plan.packet] = jnp.concatenate([hi_rows, lo_rows], axis=0)
+
+    def ahead(source, m, slot, k):
+        return pltpu.make_async_remote_copy(
+            src_ref=source.at[m],
+            dst_ref=brecv.at[m, slot],
+            send_sem=b_send.at[m, slot],
+            recv_sem=b_recv.at[m, slot],
+            device_id={"sz": iz + k},
+            device_id_type=pl.DeviceIdType.MESH,
+        )
+
+    jumps = [(0, 1), (1, 1), (2, 3)]
+    b_copies = [
+        [ahead(tsend if slot == 0 else usend, m, slot, k) for slot, k in jumps] for m in range(BATCH)
+    ]
+
+    def goes(k):
+        return iz + k < plan.planes
+
+    def plane_total(m):
         for copy in a_copies[m]:
             copy.wait_recv()
         total = jnp.zeros((plan.shard, DSTATE), F32)
@@ -474,51 +485,48 @@
         for d in range(ring):
             pref[m, d] = total
             qpref[m, d] = product
-            packet = arecv[m, d].astype(F32)
-            gates = (
-                packet[plan.shard : plan.shard + plan.gate_rows]
-                + packet[plan.shard + plan.gate_rows :]
-            )
-            total = spread(gates, plan) * total + packet[0 : plan.shard]
+            fresh, gates = unpack(arecv[m, d])
+            total = spread(gates, plan) * total + fresh
             product = product * gates
-        tsend[m, 0 : plan.shard] = total.astype(BF16)
-        hi_rows, lo_rows = split_two(product)
-        tsend[m, plan.shard : plan.packet] = jnp.concatenate([hi_rows, lo_rows], axis=0)
-        copies = []
-        if m == 0 and plan.reach >= 4:
-            hear_word(4)
-        for k in range(1, plan.reach + 1):
-            copy = pltpu.make_async_remote_copy(
-                src_ref=tsend.at[m],
-                dst_ref=brecv.at[m, k - 1],
-                send_sem=b_send.at[m, k - 1],
-                recv_sem=b_recv.at[m, k - 1],
-                device_id={"sz": iz + k},
-                device_id_type=pl.DeviceIdType.MESH,
-            )
-            pl.when(iz + k < plan.planes)(copy.start)
-            copies.append(copy)
-        b_copies.append(copies)
-
-    turn_weights()
+        pack(tsend, m, total, product)
+        ptot[m] = total
+        qtot[m] = product
+        pl.when(has_above)(b_copies[m][0].start)
+
+    def two_planes(m):
+        pl.when(has_below)(b_copies[m][0].wait_recv)
+        lower, gates = unpack(brecv[m, 0])
+        lower = jnp.where(has_below, lower, 0.0)
+        gates = jnp.where(has_below, gates, 0.0)
+        product = qtot[m]
+        pack(usend, m, spread(product, plan) * lower + ptot[m], product * gates)
+        pl.when(has_above)(b_copies[m][1].start)
+        pl.when(goes(3))(b_copies[m][2].start)
+
+    gate_inputs(0)
+    scores_of(0)
+    pl.when(goes(2))(lambda: pl.semaphore_wait(word.at[0], 1))
+    pl.when(has_below & goes(2))(lambda: tell_below(1))
     inner_of(0)
     gate_both(0)
+    plane_total(0)
+    plane_total(1)
+    scores_of(1)
     inner_of(1)
+    pl.when(goes(3))(lambda: pl.semaphore_wait(word.at[1], 1))
+    two_planes(0)
+    two_planes(1)
+    gate_inputs(1)
     gate_both(1)
+    turn_weights()
     c_copies = []
     for m in range(BATCH):
-        for k in range(plan.reach, 0, -1):
-            pl.when(iz >= k)(b_copies[m][k - 1].wait_recv)
-        incoming = jnp.zeros((plan.shard, DSTATE), F32)
-        for k in range(plan.reach, 0, -1):
-            packet = brecv[m, k - 1].astype(F32)
-            gates = (
-                packet[plan.shard : plan.shard + plan.gate_rows]
-                + packet[plan.shard + plan.gate_rows :]
-            )
-            fresh = jnp.where(iz >= k, packet[0 : plan.shard], 0.0)
-            incoming = spread(gates, plan) * incoming + fresh
-            incoming = jnp.where(iz >= k, incoming, 0.0)
+        pl.when(has_below)(b_copies[m][1].wait_recv)
+        pl.when(iz >= 3)(b_copies[m][2].wait_recv)
+        near, gates = unpack(brecv[m, 1])
+        remote, _ = unpack(brecv[m, 2])
+        incoming = spread(gates, plan) * jnp.where(iz >= 3, remote, 0.0) + near
+        incoming = jnp.where(has_below, incoming, 0.0)
         for d in range(ring):
             entering = pref[m, d] + spread(qpref[m, d], plan) * incoming
             hsend[m, d] = entering.astype(BF16)
@@ -655,8 +663,8 @@
         for copy in group:
             copy.wait_send()
     for m in range(BATCH):
-        for k in range(1, plan.reach + 1):
-            pl.when(iz + k < plan.planes)(b_copies[m][k - 1].wait_send)
+        for slot, k in jumps:
+            pl.when(goes(k))(b_copies[m][slot].wait_send)
 
 
 def shards(
@@ -681,7 +689,6 @@
     ch, ring, members = plan.channels, plan.ring, plan.members
     chunks = 2 * BATCH
     dma = pltpu.SemaphoreType.DMA
-    reach = max(plan.reach, 1)
     scratch = [
         pltpu.VMEM((BATCH, LENGTH, plan.conv), BF16),
         pltpu.VMEM((BATCH, HALO, plan.conv), BF16),
@@ -704,7 +711,10 @@
         pltpu.VMEM((BATCH, ring, plan.shard, DSTATE), F32),
         pltpu.VMEM((BATCH, ring, plan.gate_rows, DSTATE), F32),
         pltpu.VMEM((BATCH, plan.packet, DSTATE), BF16),
-        pltpu.VMEM((BATCH, reach, plan.packet, DSTATE), BF16),
+        pltpu.VMEM((BATCH, plan.packet, DSTATE), BF16),
+        pltpu.VMEM((BATCH, plan.shard, DSTATE), F32),
+        pltpu.VMEM((BATCH, plan.gate_rows, DSTATE), F32),
+        pltpu.VMEM((BATCH, 3, plan.packet, DSTATE), BF16),
         pltpu.VMEM((BATCH, ring, plan.shard, DSTATE), BF16),
         pltpu.VMEM((BATCH, ch, DSTATE), BF16),
         pltpu.VMEM((chunks, members, plan.out, HALF), BF16),
@@ -717,8 +727,8 @@
         dma((BATCH + 1,)),
         dma((BATCH, ring)),
         dma((BATCH, ring)),
-        dma((BATCH, reach)),
-        dma((BATCH, reach)),
+        dma((BATCH, 3)),
+        dma((BATCH, 3)),
         dma((BATCH, ring)),
         dma((BATCH, ring)),
         dma((BATCH, members)),
@@ -727,7 +737,7 @@
         dma((chunks, plan.far)),
         dma((chunks, plan.far)),
         dma((chunks, plan.far)),
-        pltpu.SemaphoreType.REGULAR((5,)),
+        pltpu.SemaphoreType.REGULAR((2,)),
     ]
     out = pl.pallas_call(
         functools.partial(layer_kernel, plan),

time: 59.5 us -> 58.7 us (0.987)
  the two profiles are of different devices: /device:TPU:384 before, /device:TPU:449 now
where the time goes in v5:
time: 58.7 us; the launch traced here: 57.6 us
  Pallas kernels  56.8 us (97%)
  local copies, waits for them, and re-layouts  0.73 us (1%)
    pallas_call x1, Pallas kernels, shards(): pl.pallas_call(functools.partial(layer_kernel, plan), name='mixer_layer',...  56.8 us

profile of v5, /device:TPU:449, one launch (start us, length us, event | category | flops | bytes accessed | tf_op | source)
XLA Modules:
  0.0 57.6 jit_solution(18323310554178215681)
XLA Ops:
  0.0 56.8 %mixer_layer.1 = bf16[2,320,256]{2,1,0:T(8,128)(2,1)S(1)} custom-call(bf16[2,256,640]{2,1,0:T(8,128)(2,1)} %x_hbm.1, bf16[2,256,640]{2,1,0:T(8,128)(2,1)} %z_hbm.1, bf16[2,256,128]{2,1,0:T(8,128)(2,1)} %b_hbm.1, bf16[2,256,128]{2,1,0:T(8,128)(2,1)} %c_hbm.1, f32[10,2,256]{2,1,0:T(2,128)} %bitcast.3, s32[2,256]{1,0:T(2,128)} %doc_hbm.1, ...), custom_call_target="tpu_custom_call" | custom-call | tf_op jit(solution)/shard_map/mixer_layer/pallas_call | solution.py:742
  56.8 0.7 %copy.15 = bf16[2,256,320]{1,2,0:T(8,128)(2,1)} copy(bf16[2,256,320]{1,2,0:T(8,128)(2,1)S(1)} %bitcast.2) | data formatting | bytes 655360

commit v6 on v5

--- a/solution.py
+++ b/solution.py
@@ -15,6 +15,7 @@
 BATCH = 2
 LENGTH = 256
 HALF = 128
+QUARTERS = 4
 HALO = 8
 TAPS = 4
 HEADDIM = 64
@@ -537,19 +538,24 @@
         c_copies.append(copies)
         hstate[m, home] = hsend[m, rank]
 
-    def arrow(chunk, step, upward):
-        if upward:
-            owner = lax.rem(me + plan.far - step, members)
-            first, buffer, send, got, to = 0, up_recv, up_send, up_got, up
-        else:
-            owner = lax.rem(me + members - plan.far + step, members)
-            first, buffer, send, got, to = plan.out // 2, dn_recv, dn_send, dn_got, down
-        rows = pl.ds(first, plan.out // 2) if step == 0 else pl.ds(0, plan.out)
+    quarter = plan.out // QUARTERS
+
+    def hops(q, upward):
+        return plan.far if (q < QUARTERS // 2) == upward else plan.far - 1
+
+    def owner_at(distance, upward):
+        return lax.rem(me + distance if upward else me + members - distance, members)
+
+    def arrow(m, q, hop, upward):
+        buffer, send, got, to = (
+            (up_recv, up_send, up_got, up) if upward else (dn_recv, dn_send, dn_got, down)
+        )
+        rows = pl.ds(q * quarter, quarter)
         return pltpu.make_async_remote_copy(
-            src_ref=part.at[chunk, owner, rows],
-            dst_ref=buffer.at[chunk, step, rows],
-            send_sem=send.at[chunk, step],
-            recv_sem=got.at[chunk, step],
+            src_ref=part.at[m, owner_at(hops(q, upward) - hop, upward), rows],
+            dst_ref=buffer.at[m, hop, rows],
+            send_sem=send.at[m, q, hop],
+            recv_sem=got.at[m, q, hop],
             device_id=to,
             device_id_type=pl.DeviceIdType.MESH,
         )
@@ -558,11 +564,44 @@
     s_copies = []
     gain = gain_ref[...].reshape(1, ch)
 
-    def project(m, owner):
+    def project(m, distance, upward):
+        owner = owner_at(distance, upward)
         rows = pl.ds(pl.multiple_of(owner * plan.out, 16), plan.out)
-        tile = dot(wt[rows, :], gated[m], LANES).astype(BF16)
-        part[2 * m, owner] = tile[:, 0:HALF]
-        part[2 * m + 1, owner] = tile[:, HALF:LENGTH]
+        part[m, owner] = dot(wt[rows, :], gated[m], LANES).astype(BF16)
+
+    def shoot(m, hop, upward, pieces):
+        for q in pieces:
+            if hop < hops(q, upward):
+                if hop > 0:
+                    arrows[m, q, hop - 1, upward].wait_recv()
+                    buffer = up_recv if upward else dn_recv
+                    owner = owner_at(hops(q, upward) - hop, upward)
+                    rows = slice(q * quarter, (q + 1) * quarter)
+                    total = part[m, owner, rows].astype(F32) + buffer[m, hop - 1, rows].astype(F32)
+                    part[m, owner, rows] = total.astype(BF16)
+                arrows[m, q, hop, upward] = arrow(m, q, hop, upward)
+                arrows[m, q, hop, upward].start()
+
+    early, late = range(QUARTERS // 2), range(QUARTERS // 2, QUARTERS)
+
+    def first_round(m):
+        project(m, plan.far, True)
+        shoot(m, 0, True, early)
+        shoot(m, 0, False, late)
+        if plan.far > 1:
+            project(m, plan.far - 1, True)
+            shoot(m, 0, True, late)
+            project(m, plan.far - 1, False)
+            shoot(m, 0, False, early)
+
+    def next_round(m, hop):
+        if hop + 1 < plan.far:
+            project(m, plan.far - 1 - hop, True)
+            project(m, plan.far - 1 - hop, False)
+        shoot(m, hop, True, early)
+        shoot(m, hop, False, late)
+        shoot(m, hop, True, late)
+        shoot(m, hop, False, early)
 
     def carry(m):
         for copy in c_copies[m]:
@@ -574,11 +613,7 @@
             mixed = y[m, :, at] + zg[m, :, at] * outer[:, at]
             squares = squares + mixed * mixed
             gated[m, :, at] = (mixed * gain[:, at]).astype(BF16)
-        project(m, lax.rem(me + plan.far, members))
-        for chunk in (2 * m, 2 * m + 1):
-            for upward in (True, False):
-                arrows[chunk, 0, upward] = arrow(chunk, 0, upward)
-                arrows[chunk, 0, upward].start()
+        first_round(m)
         square_hi, square_lo = split_two(squares)
         ones = jnp.ones((8, 128), BF16)
         square_rows = dot(ones, square_hi, LANES) + dot(ones, square_lo, LANES)
@@ -595,64 +630,31 @@
             copy.start()
             s_copies.append(copy)
 
-    half = plan.out // 2
-
-    def ring_step(m, step):
-        owners = {
-            True: lax.rem(me + plan.far - step, members),
-            False: lax.rem(me + members - plan.far + step, members),
-        }
-        for upward in (True, False):
-            project(m, owners[upward])
-        for chunk in (2 * m, 2 * m + 1):
-            for upward in (True, False):
-                arrows[chunk, step - 1, upward].wait_recv()
-                buffer = up_recv if upward else dn_recv
-                owner = owners[upward]
-                if step == 1:
-                    rows = slice(0, half) if upward else slice(half, plan.out)
-                else:
-                    rows = slice(0, plan.out)
-                total = part[chunk, owner, rows].astype(F32) + buffer[chunk, step - 1, rows].astype(F32)
-                part[chunk, owner, rows] = total.astype(BF16)
-                arrows[chunk, step, upward] = arrow(chunk, step, upward)
-                arrows[chunk, step, upward].start()
-
     carry(0)
-    if plan.far > 1:
-        ring_step(0, 1)
     carry(1)
-    for step in range(1, plan.far):
-        if step > 1:
-            ring_step(0, step)
-        ring_step(1, step)
-    for m in range(BATCH):
-        project(m, me)
+    for hop in range(1, plan.far):
+        for m in range(BATCH):
+            next_round(m, hop)
+    for m in range(BATCH):
+        project(m, 0, True)
 
     for copy in s_copies:
         copy.wait_recv()
-    last = plan.far - 1
     for m in range(BATCH):
         square = ssend[m]
         for k in range(1, members):
             square = square + srecv[m, k]
         scale = lax.rsqrt(square / INNER + EPSILON)
-        for side in range(2):
-            chunk = 2 * m + side
-            total = part[chunk, me].astype(F32)
-            if last == 0:
-                arrows[chunk, last, True].wait_recv()
-                arrows[chunk, last, False].wait_recv()
-                total = total + jnp.concatenate(
-                    [up_recv[chunk, 0, 0:half], dn_recv[chunk, 0, half : plan.out]], axis=0
-                ).astype(F32)
-            else:
-                for upward in (True, False):
-                    arrows[chunk, last, upward].wait_recv()
+        for q in (*late, *early):
+            rows = slice(q * quarter, (q + 1) * quarter)
+            total = part[m, me, rows].astype(F32)
+            for upward in (True, False):
+                last = hops(q, upward) - 1
+                if last >= 0:
+                    arrows[m, q, last, upward].wait_recv()
                     buffer = up_recv if upward else dn_recv
-                    total = total + buffer[chunk, last].astype(F32)
-            at = slice(side * HALF, (side + 1) * HALF)
-            out_ref[m, :, at] = (total * scale[:, at]).astype(BF16)
+                    total = total + buffer[m, last, rows].astype(F32)
+            out_ref[m, rows, :] = (total * scale).astype(BF16)
 
     def sent():
         for copy in halos:
@@ -687,7 +689,6 @@
     smem = pl.BlockSpec(memory_space=pltpu.SMEM)
     vmem = pl.BlockSpec(memory_space=pltpu.VMEM)
     ch, ring, members = plan.channels, plan.ring, plan.members
-    chunks = 2 * BATCH
     dma = pltpu.SemaphoreType.DMA
     scratch = [
         pltpu.VMEM((BATCH, LENGTH, plan.conv), BF16),
@@ -717,9 +718,9 @@
         pltpu.VMEM((BATCH, 3, plan.packet, DSTATE), BF16),
         pltpu.VMEM((BATCH, ring, plan.shard, DSTATE), BF16),
         pltpu.VMEM((BATCH, ch, DSTATE), BF16),
-        pltpu.VMEM((chunks, members, plan.out, HALF), BF16),
-        pltpu.VMEM((chunks, plan.far, plan.out, HALF), BF16),
-        pltpu.VMEM((chunks, plan.far, plan.out, HALF), BF16),
+        pltpu.VMEM((BATCH, members, plan.out, LENGTH), BF16),
+        pltpu.VMEM((BATCH, plan.far, plan.out, LENGTH), BF16),
+        pltpu.VMEM((BATCH, plan.far, plan.out, LENGTH), BF16),
         pltpu.VMEM((BATCH, 1, LENGTH), F32),
         pltpu.VMEM((BATCH, members, 1, LENGTH), F32),
         dma((13,)),
@@ -733,10 +734,10 @@
         dma((BATCH, ring)),
         dma((BATCH, members)),
         dma((BATCH, members)),
-        dma((chunks, plan.far)),
-        dma((chunks, plan.far)),
-        dma((chunks, plan.far)),
-        dma((chunks, plan.far)),
+        dma((BATCH, QUARTERS, plan.far)),
+        dma((BATCH, QUARTERS, plan.far)),
+        dma((BATCH, QUARTERS, plan.far)),
+        dma((BATCH, QUARTERS, plan.far)),
         pltpu.SemaphoreType.REGULAR((2,)),
     ]
     out = pl.pallas_call(

time: 58.7 us -> 58.7 us (level); the launches traced: 57.6 us -> 58.6 us
  Pallas kernels: 56.8 us -> 57.9 us
    pallas_call x1, Pallas kernels: 56.8 us -> 57.9 us  [shards(): pl.pallas_call(functools.partial(layer_kernel, plan), name='mixer_layer',...]
where the time goes in v6:
time: 58.7 us; the launch traced here: 58.6 us
  Pallas kernels  57.9 us (99%)
  local copies, waits for them, and re-layouts  0.73 us (1%)
    pallas_call x1, Pallas kernels, shards(): pl.pallas_call(functools.partial(layer_kernel, plan), name='mixer_layer',...  57.9 us

profile of v6, /device:TPU:449, one launch (start us, length us, event | category | flops | bytes accessed | tf_op | source)
XLA Modules:
  0.0 58.6 jit_solution(8466890312262385944)
XLA Ops:
  0.0 57.9 %mixer_layer.1 = bf16[2,320,256]{2,1,0:T(8,128)(2,1)S(1)} custom-call(bf16[2,256,640]{2,1,0:T(8,128)(2,1)} %x_hbm.1, bf16[2,256,640]{2,1,0:T(8,128)(2,1)} %z_hbm.1, bf16[2,256,128]{2,1,0:T(8,128)(2,1)} %b_hbm.1, bf16[2,256,128]{2,1,0:T(8,128)(2,1)} %c_hbm.1, f32[10,2,256]{2,1,0:T(2,128)} %bitcast.3, s32[2,256]{1,0:T(2,128)} %doc_hbm.1, ...), custom_call_target="tpu_custom_call" | custom-call | tf_op jit(solution)/shard_map/mixer_layer/pallas_call | solution.py:743
  57.9 0.7 %copy.15 = bf16[2,256,320]{1,2,0:T(8,128)(2,1)} copy(bf16[2,256,320]{1,2,0:T(8,128)(2,1)S(1)} %bitcast.2) | data formatting | bytes 655360

commit v7 on v6

--- a/solution.py
+++ b/solution.py
@@ -82,11 +82,14 @@
     cx_hbm,
     cb_hbm,
     cc_hbm,
+    bias_hbm,
+    rate_hbm,
+    gain_hbm,
+    w_hbm,
+    out_ref,
     bias_ref,
     rate_ref,
     gain_ref,
-    w_hbm,
-    out_ref,
     xbc,
     halo,
     docs_ref,
@@ -199,13 +202,7 @@
         for copy in loads:
             need(copy)
 
-    got_dt = load(dt_hbm, dt_ref)
     got_docs = load(doc_hbm, docs_ref)
-    got_taps = [
-        load(cx_hbm, taps.at[:, pl.ds(0, ch)]),
-        load(cb_hbm, taps.at[:, pl.ds(ch, DSTATE)]),
-        load(cc_hbm, taps.at[:, pl.ds(ch + DSTATE, DSTATE)]),
-    ]
     got_rows = []
     for m in range(BATCH):
         got_rows.append(
@@ -215,6 +212,13 @@
                 load(c_hbm.at[m], xbc.at[m, :, pl.ds(ch + DSTATE, DSTATE)]),
             ]
         )
+    got_dt = [load(dt_hbm, dt_ref), load(bias_hbm, bias_ref), load(rate_hbm, rate_ref)]
+    got_taps = [
+        load(cx_hbm, taps.at[:, pl.ds(0, ch)]),
+        load(cb_hbm, taps.at[:, pl.ds(ch, DSTATE)]),
+        load(cc_hbm, taps.at[:, pl.ds(ch + DSTATE, DSTATE)]),
+    ]
+    got_gain = load(gain_hbm, gain_ref)
     got_z = load(z_hbm, z_ref)
     got_w = load(w_hbm, w_ref)
 
@@ -266,7 +270,8 @@
         for k in range(1, TAPS):
             at = m * TAPS + k
             masks[m, k - 1] = jnp.broadcast_to(mark_cols[:, at : at + 1], (LENGTH, 128))
-    need(got_dt)
+    for copy in got_dt:
+        need(copy)
     head_row = lax.broadcasted_iota(jnp.int32, (16, LENGTH), 0)
     bias = jnp.zeros((16, LENGTH), F32)
     rate = jnp.zeros((16, LENGTH), F32)
@@ -562,6 +567,7 @@
 
     arrows = {}
     s_copies = []
+    need(got_gain)
     gain = gain_ref[...].reshape(1, ch)
 
     def project(m, distance, upward):
@@ -686,11 +692,13 @@
     w_out,
 ):
     hbm = pl.BlockSpec(memory_space=pltpu.HBM)
-    smem = pl.BlockSpec(memory_space=pltpu.SMEM)
     vmem = pl.BlockSpec(memory_space=pltpu.VMEM)
     ch, ring, members = plan.channels, plan.ring, plan.members
     dma = pltpu.SemaphoreType.DMA
     scratch = [
+        pltpu.SMEM((plan.heads,), F32),
+        pltpu.SMEM((plan.heads,), F32),
+        pltpu.VMEM((ch,), F32),
         pltpu.VMEM((BATCH, LENGTH, plan.conv), BF16),
         pltpu.VMEM((BATCH, HALO, plan.conv), BF16),
         pltpu.VMEM((BATCH, LENGTH), jnp.int32),
@@ -723,7 +731,7 @@
         pltpu.VMEM((BATCH, plan.far, plan.out, LENGTH), BF16),
         pltpu.VMEM((BATCH, 1, LENGTH), F32),
         pltpu.VMEM((BATCH, members, 1, LENGTH), F32),
-        dma((13,)),
+        dma((16,)),
         dma((BATCH + 1,)),
         dma((BATCH + 1,)),
         dma((BATCH, ring)),
@@ -744,7 +752,7 @@
         functools.partial(layer_kernel, plan),
         name="mixer_layer",
         out_shape=pltpu.VMEM((BATCH, plan.out, LENGTH), BF16),
-        in_specs=[hbm] * 9 + [smem, smem, vmem, hbm],
+        in_specs=[hbm] * 13,
         out_specs=vmem,
         scratch_shapes=scratch,
         compiler_params=pltpu.CompilerParams(

time: 58.7 us -> 57.2 us (0.974)
  Pallas kernels: 57.9 us -> 56.4 us
    pallas_call x1, Pallas kernels: 57.9 us -> 56.4 us  [shards(): pl.pallas_call(functools.partial(layer_kernel, plan), name='mixer_layer',...]
where the time goes in v7:
time: 57.2 us; the launch traced here: 57.1 us
  Pallas kernels  56.4 us (99%)
  local copies, waits for them, and re-layouts  0.73 us (1%)
    pallas_call x1, Pallas kernels, shards(): pl.pallas_call(functools.partial(layer_kernel, plan), name='mixer_layer',...  56.4 us

profile of v7, /device:TPU:449, one launch (start us, length us, event | category | flops | bytes accessed | tf_op | source)
XLA Modules:
  0.0 57.1 jit_solution(13187545926639864941)
XLA Ops:
  0.0 56.4 %mixer_layer.1 = bf16[2,320,256]{2,1,0:T(8,128)(2,1)S(1)} custom-call(bf16[2,256,640]{2,1,0:T(8,128)(2,1)} %x_hbm.1, bf16[2,256,640]{2,1,0:T(8,128)(2,1)} %z_hbm.1, bf16[2,256,128]{2,1,0:T(8,128)(2,1)} %b_hbm.1, bf16[2,256,128]{2,1,0:T(8,128)(2,1)} %c_hbm.1, f32[10,2,256]{2,1,0:T(2,128)} %bitcast.3, s32[2,256]{1,0:T(2,128)} %doc_hbm.1, ...), custom_call_target="tpu_custom_call" | custom-call | tf_op jit(solution)/shard_map/mixer_layer/pallas_call | solution.py:751
  56.4 0.7 %copy.15 = bf16[2,256,320]{1,2,0:T(8,128)(2,1)} copy(bf16[2,256,320]{1,2,0:T(8,128)(2,1)S(1)} %bitcast.2) | data formatting | bytes 655360

commit v8 on v7

--- a/solution.py
+++ b/solution.py
@@ -101,6 +101,7 @@
     wt,
     conv,
     masks,
+    main_state,
     xw,
     y,
     scores,
@@ -219,12 +220,12 @@
         load(cc_hbm, taps.at[:, pl.ds(ch + DSTATE, DSTATE)]),
     ]
     got_gain = load(gain_hbm, gain_ref)
-    got_z = load(z_hbm, z_ref)
-    got_w = load(w_hbm, w_ref)
 
     need(got_docs)
     for copy in (*got_rows[0], *got_rows[1]):
         need(copy)
+    got_z = load(z_hbm, z_ref)
+    got_w = load(w_hbm, w_ref)
     pl.semaphore_wait(barrier, count)
     pl.when(has_below & has_above)(lambda: tell_below(0))
 
@@ -330,6 +331,8 @@
             if j < plan.pairs:
                 scale = pair_columns(cols, weight_col + m * 16 + 2 * j, lane)
                 xw[m, :, at] = (total.astype(BF16).astype(F32) * scale).astype(BF16)
+        xw[m, 0:HALO, :] = jnp.zeros((HALO, ch), BF16)
+        main_state[m] = dot(xw[m], conv[m, :, ch : ch + DSTATE], ROWS)
 
     def turn_weights():
         need(got_w)
@@ -342,18 +345,29 @@
             at = slice(j * 128, (j + 1) * 128)
             zg[m, :, at] = silu(z_ref[m, :, at].astype(F32))
 
+    group_row = lax.broadcasted_iota(jnp.int32, (ring * plan.gate_rows, 16), 0)
+    group_head = lax.broadcasted_iota(jnp.int32, (ring * plan.gate_rows, 16), 1)
+    bits = plan.gate_rows.bit_length() - 1
+    shard_of, group_of = group_row >> bits, group_row & (plan.gate_rows - 1)
+    picks = (((shard_of * plan.groups + group_of) >> 2) == group_head) & (group_of < plan.groups)
+    pick = jnp.where(picks, 1.0, 0.0).astype(BF16)
+    plain = (((1,), (0,)), ((), ()))
+    gate_parts = []
+    for m in range(BATCH):
+        gate_hi, gate_lo = split_two(jnp.broadcast_to(jnp.exp(ends[m]), (16, DSTATE)))
+        gate_parts.append((dot(pick, gate_hi, plain), dot(pick, gate_lo, plain)))
     convolve(0)
     pl.when(has_prior)(halos[BATCH].wait_recv)
     doc_before = jnp.where(has_prior, doc_halo[...].astype(F32), -1.0)
-    edge_marks = []
-    joined = jnp.concatenate([doc_before, docs[:, 0:128]], axis=1)
-    for k in range(1, TAPS):
-        edge_marks.append(jnp.where(pltpu.roll(joined, k, 1) == joined, 1.0, 0.0))
-    edge_rows = jnp.concatenate(
-        edge_marks + [jnp.zeros((16 - BATCH * (TAPS - 1), LENGTH), F32)], axis=0
-    )[:, 128:256]
-    edge_rows = jnp.concatenate([edge_rows, jnp.zeros((112, 128), F32)], axis=0)
-    edge_cols = edge_rows.T[0:HALO]
+    row8 = lax.broadcasted_iota(jnp.int32, (HALO, 128), 0)
+
+    def edge_mask(m, k):
+        mask = masks[m, k - 1, 0:HALO]
+        for t in range(k):
+            at = 128 - k + t
+            same = docs[m : m + 1, t : t + 1] == doc_before[m : m + 1, at : at + 1]
+            mask = jnp.where(row8 == t, jnp.where(same, 1.0, 0.0), mask)
+        return mask
 
     def exchange(m, source, target, peers_send, peers_recv):
         copies = []
@@ -371,17 +385,13 @@
             )
         return copies
 
-    group_row = lax.broadcasted_iota(jnp.int32, (ring * plan.gate_rows, 16), 0)
-    group_head = lax.broadcasted_iota(jnp.int32, (ring * plan.gate_rows, 16), 1)
-    bits = plan.gate_rows.bit_length() - 1
-    shard_of, group_of = group_row >> bits, group_row & (plan.gate_rows - 1)
-    picks = (((shard_of * plan.groups + group_of) >> 2) == group_head) & (group_of < plan.groups)
-    pick = jnp.where(picks, 1.0, 0.0).astype(BF16)
     a_copies = []
     for m in range(BATCH):
         if m > 0:
             convolve(m)
         pl.when(has_prior)(halos[m].wait_recv)
+        same = [None, *(edge_mask(m, k) for k in range(1, TAPS))]
+        scaled = []
         for j in range(tiles):
             at = slice(j * 128, (j + 1) * 128)
             lead = jnp.where(has_prior, halo[m, :, at].astype(F32), 0.0)
@@ -390,20 +400,20 @@
             total = own * tap[TAPS - 1 : TAPS, at]
             for k in range(1, TAPS):
                 weight = tap[TAPS - 1 - k : TAPS - k, at]
-                same = edge_cols[:, (k - 1) * BATCH + m : (k - 1) * BATCH + m + 1]
-                total = total + (pltpu.roll(both, k, 0)[HALO : 2 * HALO] * weight) * same
-            total = silu(total)
-            conv[m, 0:HALO, at] = total.astype(BF16)
+                total = total + (pltpu.roll(both, k, 0)[HALO : 2 * HALO] * weight) * same[k]
+            total = silu(total).astype(BF16)
+            conv[m, 0:HALO, at] = total
             if j < plan.pairs:
                 scale = pair_columns(cols[0:HALO], weight_col + m * 16 + 2 * j, lane[0:HALO])
-                xw[m, 0:HALO, at] = (total.astype(BF16).astype(F32) * scale).astype(BF16)
-        state = dot(xw[m], conv[m, :, ch : ch + DSTATE], ROWS).astype(BF16)
+                scaled.append((total.astype(F32) * scale).astype(BF16))
+            if j == plan.pairs:
+                first_b = total
+        edge_state = dot(jnp.concatenate(scaled, axis=1), first_b, ROWS)
+        state = (main_state[m] + edge_state).astype(BF16)
         carried_end = docs[m : m + 1, LENGTH - 1 : LENGTH] == doc_before[m : m + 1, 127:128]
-        gate = jnp.broadcast_to(jnp.exp(ends[m]) * jnp.where(carried_end, 1.0, 0.0), (16, DSTATE))
-        gate_hi, gate_lo = split_two(gate)
-        plain = (((1,), (0,)), ((), ()))
-        hi_rows = dot(pick, gate_hi, plain).astype(BF16)
-        lo_rows = dot(pick, gate_lo, plain).astype(BF16)
+        carried_end = jnp.where(carried_end, 1.0, 0.0)
+        hi_rows = (gate_parts[m][0] * carried_end).astype(BF16)
+        lo_rows = (gate_parts[m][1] * carried_end).astype(BF16)
         for r in range(ring):
             fsend[m, r, 0 : plan.shard] = state[r * plan.shard : (r + 1) * plan.shard]
             at = slice(r * plan.gate_rows, (r + 1) * plan.gate_rows)
@@ -710,6 +720,7 @@
         pltpu.VMEM((plan.width, ch), BF16),
         pltpu.VMEM((BATCH, LENGTH, plan.conv), BF16),
         pltpu.VMEM((BATCH, TAPS - 1, LENGTH, 128), F32),
+        pltpu.VMEM((BATCH, ch, DSTATE), F32),
         pltpu.VMEM((BATCH, LENGTH, ch), BF16),
         pltpu.VMEM((BATCH, LENGTH, ch), F32),
         pltpu.VMEM((BATCH, LENGTH, LENGTH), F32),

time: 57.2 us -> 57.5 us (level)
  no operation moved by 1% of the time
where the time goes in v8:
time: 57.5 us; the launch traced here: 57.4 us
  Pallas kernels  56.7 us (99%)
  local copies, waits for them, and re-layouts  0.73 us (1%)
    pallas_call x1, Pallas kernels, shards(): pl.pallas_call(functools.partial(layer_kernel, plan), name='mixer_layer',...  56.7 us

profile of v8, /device:TPU:449, one launch (start us, length us, event | category | flops | bytes accessed | tf_op | source)
XLA Modules:
  0.0 57.4 jit_solution(9735139222926503762)
XLA Ops:
  0.0 56.7 %mixer_layer.1 = bf16[2,320,256]{2,1,0:T(8,128)(2,1)S(1)} custom-call(bf16[2,256,640]{2,1,0:T(8,128)(2,1)} %x_hbm.1, bf16[2,256,640]{2,1,0:T(8,128)(2,1)} %z_hbm.1, bf16[2,256,128]{2,1,0:T(8,128)(2,1)} %b_hbm.1, bf16[2,256,128]{2,1,0:T(8,128)(2,1)} %c_hbm.1, f32[10,2,256]{2,1,0:T(2,128)} %bitcast.3, s32[2,256]{1,0:T(2,128)} %doc_hbm.1, ...), custom_call_target="tpu_custom_call" | custom-call | tf_op jit(solution)/shard_map/mixer_layer/pallas_call | solution.py:762
  56.7 0.7 %copy.15 = bf16[2,256,320]{1,2,0:T(8,128)(2,1)} copy(bf16[2,256,320]{1,2,0:T(8,128)(2,1)S(1)} %bitcast.2) | data formatting | bytes 655360

commit v9 on v8

--- a/solution.py
+++ b/solution.py
@@ -169,10 +169,10 @@
 
     for k in range(1, ring):
         greet(in_plane(lax.rem(rank + k, ring)))
-    for k in range(1, members):
-        greet({"mp": lax.rem(me + k, members)})
+    greet(up)
+    greet(down)
     pl.when(has_prior)(lambda: greet(prior))
-    count = ring - 1 + members - 1 + one(has_next)
+    count = ring - 1 + 2 + one(has_next)
     above, below = {"sz": iz + 1}, {"sz": iz - 1}
     has_above, has_below = iz + 1 < plan.planes, iz > 0
     pl.when(has_below)(lambda: greet(below))
@@ -576,7 +576,7 @@
         )
 
     arrows = {}
-    s_copies = []
+    square_copies = {}
     need(got_gain)
     gain = gain_ref[...].reshape(1, ch)
 
@@ -610,6 +610,22 @@
             project(m, plan.far - 1, False)
             shoot(m, 0, False, early)
 
+    def pass_squares(m, hop):
+        for side, upward in enumerate((True, False)):
+            if hop < (plan.far if upward else plan.far - 1):
+                if hop > 0:
+                    square_copies[m, hop - 1, upward].wait_recv()
+                copy = pltpu.make_async_remote_copy(
+                    src_ref=ssend.at[m] if hop == 0 else srecv.at[m, side, hop - 1],
+                    dst_ref=srecv.at[m, side, hop],
+                    send_sem=s_send.at[m, side, hop],
+                    recv_sem=s_recv.at[m, side, hop],
+                    device_id=up if upward else down,
+                    device_id_type=pl.DeviceIdType.MESH,
+                )
+                copy.start()
+                square_copies[m, hop, upward] = copy
+
     def next_round(m, hop):
         if hop + 1 < plan.far:
             project(m, plan.far - 1 - hop, True)
@@ -618,6 +634,7 @@
         shoot(m, hop, False, late)
         shoot(m, hop, True, late)
         shoot(m, hop, False, early)
+        pass_squares(m, hop)
 
     def carry(m):
         for copy in c_copies[m]:
@@ -634,17 +651,7 @@
         ones = jnp.ones((8, 128), BF16)
         square_rows = dot(ones, square_hi, LANES) + dot(ones, square_lo, LANES)
         ssend[m] = square_rows[0:1]
-        for k in range(1, members):
-            copy = pltpu.make_async_remote_copy(
-                src_ref=ssend.at[m],
-                dst_ref=srecv.at[m, k],
-                send_sem=s_send.at[m, k],
-                recv_sem=s_recv.at[m, k],
-                device_id={"mp": lax.rem(me + k, members)},
-                device_id_type=pl.DeviceIdType.MESH,
-            )
-            copy.start()
-            s_copies.append(copy)
+        pass_squares(m, 0)
 
     carry(0)
     carry(1)
@@ -654,12 +661,14 @@
     for m in range(BATCH):
         project(m, 0, True)
 
-    for copy in s_copies:
-        copy.wait_recv()
     for m in range(BATCH):
         square = ssend[m]
-        for k in range(1, members):
-            square = square + srecv[m, k]
+        for side, upward in enumerate((True, False)):
+            last = (plan.far if upward else plan.far - 1) - 1
+            if last >= 0:
+                square_copies[m, last, upward].wait_recv()
+            for hop in range(last + 1):
+                square = square + srecv[m, side, hop]
         scale = lax.rsqrt(square / INNER + EPSILON)
         for q in (*late, *early):
             rows = slice(q * quarter, (q + 1) * quarter)
@@ -677,7 +686,7 @@
             copy.wait_send()
 
     pl.when(has_next)(sent)
-    for group in (*a_copies, *c_copies, s_copies, list(arrows.values())):
+    for group in (*a_copies, *c_copies, list(square_copies.values()), list(arrows.values())):
         for copy in group:
             copy.wait_send()
     for m in range(BATCH):
@@ -741,7 +750,7 @@
         pltpu.VMEM((BATCH, plan.far, plan.out, LENGTH), BF16),
         pltpu.VMEM((BATCH, plan.far, plan.out, LENGTH), BF16),
         pltpu.VMEM((BATCH, 1, LENGTH), F32),
-        pltpu.VMEM((BATCH, members, 1, LENGTH), F32),
+        pltpu.VMEM((BATCH, 2, plan.far, 1, LENGTH), F32),
         dma((16,)),
         dma((BATCH + 1,)),
         dma((BATCH + 1,)),
@@ -751,8 +760,8 @@
         dma((BATCH, 3)),
         dma((BATCH, ring)),
         dma((BATCH, ring)),
-        dma((BATCH, members)),
-        dma((BATCH, members)),
+        dma((BATCH, 2, plan.far)),
+        dma((BATCH, 2, plan.far)),
         dma((BATCH, QUARTERS, plan.far)),
         dma((BATCH, QUARTERS, plan.far)),
         dma((BATCH, QUARTERS, plan.far)),

time: 57.5 us -> 57.4 us (level)
  no operation moved by 1% of the time
where the time goes in v9:
time: 57.4 us; the launch traced here: 56.9 us
  Pallas kernels  56.2 us (98%)
  local copies, waits for them, and re-layouts  0.73 us (1%)
    pallas_call x1, Pallas kernels, shards(): pl.pallas_call(functools.partial(layer_kernel, plan), name='mixer_layer',...  56.2 us

profile of v9, /device:TPU:449, one launch (start us, length us, event | category | flops | bytes accessed | tf_op | source)
XLA Modules:
  0.0 56.9 jit_solution(476453539803144527)
XLA Ops:
  0.0 56.2 %mixer_layer.1 = bf16[2,320,256]{2,1,0:T(8,128)(2,1)S(1)} custom-call(bf16[2,256,640]{2,1,0:T(8,128)(2,1)} %x_hbm.1, bf16[2,256,640]{2,1,0:T(8,128)(2,1)} %z_hbm.1, bf16[2,256,128]{2,1,0:T(8,128)(2,1)} %b_hbm.1, bf16[2,256,128]{2,1,0:T(8,128)(2,1)} %c_hbm.1, f32[10,2,256]{2,1,0:T(2,128)} %bitcast.3, s32[2,256]{1,0:T(2,128)} %doc_hbm.1, ...), custom_call_target="tpu_custom_call" | custom-call | tf_op jit(solution)/shard_map/mixer_layer/pallas_call | solution.py:771
  56.2 0.7 %copy.15 = bf16[2,256,320]{1,2,0:T(8,128)(2,1)} copy(bf16[2,256,320]{1,2,0:T(8,128)(2,1)S(1)} %bitcast.2) | data formatting | bytes 655360

commit v10 on v9

--- a/solution.py
+++ b/solution.py
@@ -15,7 +15,7 @@
 BATCH = 2
 LENGTH = 256
 HALF = 128
-QUARTERS = 4
+QUARTERS = 2
 HALO = 8
 TAPS = 4
 HEADDIM = 64
@@ -134,9 +134,8 @@
     c_recv,
     s_send,
     s_recv,
-    up_send,
+    ring_send,
     up_got,
-    dn_send,
     dn_got,
     word,
 ):
@@ -186,11 +185,19 @@
 
     loads = []
 
-    def load(src, dst):
-        copy = pltpu.make_async_copy(src, dst, load_sem.at[len(loads)])
+    def load(src, dst, sem=None):
+        copy = pltpu.make_async_copy(src, dst, load_sem.at[len(loads) if sem is None else sem])
         copy.start()
-        loads.append(copy)
+        if sem is None:
+            loads.append(copy)
         return copy
+
+    def load_group(copies, whole):
+        sem = len(loads)
+        for src, dst in copies:
+            load(src, dst, sem)
+        loads.append(pltpu.make_async_copy(whole, whole, load_sem.at[sem]))
+        return loads[-1]
 
     done = []
 
@@ -204,26 +211,27 @@
             need(copy)
 
     got_docs = load(doc_hbm, docs_ref)
-    got_rows = []
-    for m in range(BATCH):
-        got_rows.append(
-            [
-                load(x_hbm.at[m], xbc.at[m, :, pl.ds(0, ch)]),
-                load(b_hbm.at[m], xbc.at[m, :, pl.ds(ch, DSTATE)]),
-                load(c_hbm.at[m], xbc.at[m, :, pl.ds(ch + DSTATE, DSTATE)]),
-            ]
-        )
+    row_parts = []
+    for m in range(BATCH):
+        row_parts += [
+            (x_hbm.at[m], xbc.at[m, :, pl.ds(0, ch)]),
+            (b_hbm.at[m], xbc.at[m, :, pl.ds(ch, DSTATE)]),
+            (c_hbm.at[m], xbc.at[m, :, pl.ds(ch + DSTATE, DSTATE)]),
+        ]
+    got_rows = load_group(row_parts, xbc)
     got_dt = [load(dt_hbm, dt_ref), load(bias_hbm, bias_ref), load(rate_hbm, rate_ref)]
-    got_taps = [
-        load(cx_hbm, taps.at[:, pl.ds(0, ch)]),
-        load(cb_hbm, taps.at[:, pl.ds(ch, DSTATE)]),
-        load(cc_hbm, taps.at[:, pl.ds(ch + DSTATE, DSTATE)]),
-    ]
+    got_taps = load_group(
+        [
+            (cx_hbm, taps.at[:, pl.ds(0, ch)]),
+            (cb_hbm, taps.at[:, pl.ds(ch, DSTATE)]),
+            (cc_hbm, taps.at[:, pl.ds(ch + DSTATE, DSTATE)]),
+        ],
+        taps,
+    )
     got_gain = load(gain_hbm, gain_ref)
 
     need(got_docs)
-    for copy in (*got_rows[0], *got_rows[1]):
-        need(copy)
+    need(got_rows)
     got_z = load(z_hbm, z_ref)
     got_w = load(w_hbm, w_ref)
     pl.semaphore_wait(barrier, count)
@@ -314,8 +322,7 @@
     cols = jnp.concatenate(row_mats, axis=0).T
     log_col, weight_col, entry_col = 0, span, 2 * span
 
-    for copy in got_taps:
-        need(copy)
+    need(got_taps)
     tap = taps[...].astype(F32)
     tiles = plan.conv // 128
     def convolve(m):
@@ -377,13 +384,23 @@
                 pltpu.make_async_remote_copy(
                     src_ref=source.at[m, to],
                     dst_ref=target(to),
-                    send_sem=peers_send.at[m, k],
-                    recv_sem=peers_recv.at[m, k],
+                    send_sem=peers_send.at[m],
+                    recv_sem=peers_recv.at[m],
                     device_id=in_plane(to),
                     device_id_type=pl.DeviceIdType.MESH,
                 )
             )
         return copies
+
+    def all_of(m, ref, send_sem, recv_sem):
+        return pltpu.make_async_remote_copy(
+            src_ref=ref.at[m, pl.ds(0, ring - 1)],
+            dst_ref=ref.at[m, pl.ds(0, ring - 1)],
+            send_sem=send_sem.at[m],
+            recv_sem=recv_sem.at[m],
+            device_id=in_plane(lax.rem(rank + 1, ring)),
+            device_id_type=pl.DeviceIdType.MESH,
+        )
 
     a_copies = []
     for m in range(BATCH):
@@ -423,7 +440,7 @@
         copies = exchange(m, fsend, lambda to, m=m: arecv.at[m, rank], a_send, a_recv)
         for copy in copies:
             copy.start()
-        a_copies.append(copies)
+        a_copies.append([all_of(m, arecv, a_send, a_recv)])
         arecv[m, pl.ds(rank, 1)] = fsend[m, pl.ds(rank, 1)]
 
     def scores_of(m):
@@ -550,7 +567,7 @@
         copies = exchange(m, hsend, lambda to, m=m: hstate.at[m, home], c_send, c_recv)
         for copy in copies:
             copy.start()
-        c_copies.append(copies)
+        c_copies.append([all_of(m, hsend, c_send, c_recv)])
         hstate[m, home] = hsend[m, rank]
 
     quarter = plan.out // QUARTERS
@@ -563,13 +580,15 @@
 
     def arrow(m, q, hop, upward):
         buffer, send, got, to = (
-            (up_recv, up_send, up_got, up) if upward else (dn_recv, dn_send, dn_got, down)
+            (up_recv, ring_send.at[0], up_got, up)
+            if upward
+            else (dn_recv, ring_send.at[1], dn_got, down)
         )
         rows = pl.ds(q * quarter, quarter)
         return pltpu.make_async_remote_copy(
             src_ref=part.at[m, owner_at(hops(q, upward) - hop, upward), rows],
             dst_ref=buffer.at[m, hop, rows],
-            send_sem=send.at[m, q, hop],
+            send_sem=send,
             recv_sem=got.at[m, q, hop],
             device_id=to,
             device_id_type=pl.DeviceIdType.MESH,
@@ -618,7 +637,7 @@
                 copy = pltpu.make_async_remote_copy(
                     src_ref=ssend.at[m] if hop == 0 else srecv.at[m, side, hop - 1],
                     dst_ref=srecv.at[m, side, hop],
-                    send_sem=s_send.at[m, side, hop],
+                    send_sem=s_send.at[m, side],
                     recv_sem=s_recv.at[m, side, hop],
                     device_id=up if upward else down,
                     device_id_type=pl.DeviceIdType.MESH,
@@ -686,9 +705,31 @@
             copy.wait_send()
 
     pl.when(has_next)(sent)
-    for group in (*a_copies, *c_copies, list(square_copies.values()), list(arrows.values())):
+    for group in (*a_copies, *c_copies):
         for copy in group:
             copy.wait_send()
+    sent_halves = BATCH * (2 * plan.far - 1)
+    assert QUARTERS == 2 and sent_halves % 2 == 0
+    for side, to in enumerate((up, down)):
+        pltpu.make_async_remote_copy(
+            src_ref=part.at[0, pl.ds(0, sent_halves // 2)],
+            dst_ref=part.at[0, pl.ds(0, sent_halves // 2)],
+            send_sem=ring_send.at[side],
+            recv_sem=up_got.at[0, 0, 0],
+            device_id=to,
+            device_id_type=pl.DeviceIdType.MESH,
+        ).wait_send()
+        for m in range(BATCH):
+            rows = pl.ds(0, plan.far - side)
+            if plan.far > side:
+                pltpu.make_async_remote_copy(
+                    src_ref=srecv.at[m, side, rows],
+                    dst_ref=srecv.at[m, side, rows],
+                    send_sem=s_send.at[m, side],
+                    recv_sem=s_recv.at[m, side, 0],
+                    device_id=to,
+                    device_id_type=pl.DeviceIdType.MESH,
+                ).wait_send()
     for m in range(BATCH):
         for slot, k in jumps:
             pl.when(goes(k))(b_copies[m][slot].wait_send)
@@ -751,19 +792,18 @@
         pltpu.VMEM((BATCH, plan.far, plan.out, LENGTH), BF16),
         pltpu.VMEM((BATCH, 1, LENGTH), F32),
         pltpu.VMEM((BATCH, 2, plan.far, 1, LENGTH), F32),
-        dma((16,)),
+        dma((9,)),
         dma((BATCH + 1,)),
         dma((BATCH + 1,)),
-        dma((BATCH, ring)),
-        dma((BATCH, ring)),
+        dma((BATCH,)),
+        dma((BATCH,)),
         dma((BATCH, 3)),
         dma((BATCH, 3)),
-        dma((BATCH, ring)),
-        dma((BATCH, ring)),
+        dma((BATCH,)),
+        dma((BATCH,)),
+        dma((BATCH, 2)),
         dma((BATCH, 2, plan.far)),
-        dma((BATCH, 2, plan.far)),
-        dma((BATCH, QUARTERS, plan.far)),
-        dma((BATCH, QUARTERS, plan.far)),
+        dma((2,)),
         dma((BATCH, QUARTERS, plan.far)),
         dma((BATCH, QUARTERS, plan.far)),
         pltpu.SemaphoreType.REGULAR((2,)),

time: 57.4 us -> 55.6 us (0.969)
  Pallas kernels: 56.2 us -> 54.5 us
    pallas_call x1, Pallas kernels: 56.2 us -> 54.5 us  [shards(): pl.pallas_call(functools.partial(layer_kernel, plan), name='mixer_layer',...]
where the time goes in v10:
time: 55.6 us; the launch traced here: 55.2 us
  Pallas kernels  54.5 us (98%)
  local copies, waits for them, and re-layouts  0.73 us (1%)
    pallas_call x1, Pallas kernels, shards(): pl.pallas_call(functools.partial(layer_kernel, plan), name='mixer_layer',...  54.5 us

profile of v10, /device:TPU:449, one launch (start us, length us, event | category | flops | bytes accessed | tf_op | source)
XLA Modules:
  0.0 55.2 jit_solution(3997404321003177135)
XLA Ops:
  0.0 54.5 %mixer_layer.1 = bf16[2,320,256]{2,1,0:T(8,128)(2,1)S(1)} custom-call(bf16[2,256,640]{2,1,0:T(8,128)(2,1)} %x_hbm.1, bf16[2,256,640]{2,1,0:T(8,128)(2,1)} %z_hbm.1, bf16[2,256,128]{2,1,0:T(8,128)(2,1)} %b_hbm.1, bf16[2,256,128]{2,1,0:T(8,128)(2,1)} %c_hbm.1, f32[10,2,256]{2,1,0:T(2,128)} %bitcast.3, s32[2,256]{1,0:T(2,128)} %doc_hbm.1, ...), custom_call_target="tpu_custom_call" | custom-call | tf_op jit(solution)/shard_map/mixer_layer/pallas_call | solution.py:811
  54.5 0.7 %copy.15 = bf16[2,256,320]{1,2,0:T(8,128)(2,1)} copy(bf16[2,256,320]{1,2,0:T(8,128)(2,1)S(1)} %bitcast.2) | data formatting | bytes 655360

commit v11 on v10

--- a/solution.py
+++ b/solution.py
@@ -237,30 +237,27 @@
     pl.semaphore_wait(barrier, count)
     pl.when(has_below & has_above)(lambda: tell_below(0))
 
-    halos = []
-    for m in range(BATCH):
-        halos.append(
-            pltpu.make_async_remote_copy(
-                src_ref=xbc.at[m, pl.ds(LENGTH - HALO, HALO)],
-                dst_ref=halo.at[m],
-                send_sem=halo_send.at[m],
-                recv_sem=halo_recv.at[m],
-                device_id=after,
-                device_id_type=pl.DeviceIdType.MESH,
-            )
-        )
-    halos.append(
+    halos = [
         pltpu.make_async_remote_copy(
             src_ref=docs_ref.at[:, pl.ds(LENGTH - 128, 128)],
             dst_ref=doc_halo,
-            send_sem=halo_send.at[BATCH],
-            recv_sem=halo_recv.at[BATCH],
+            send_sem=halo_send.at[0],
+            recv_sem=halo_recv.at[0],
             device_id=after,
             device_id_type=pl.DeviceIdType.MESH,
-        )
-    )
+        ),
+        pltpu.make_async_remote_copy(
+            src_ref=xbc.at[:, pl.ds(LENGTH - HALO, HALO)],
+            dst_ref=halo,
+            send_sem=halo_send.at[1],
+            recv_sem=halo_recv.at[1],
+            device_id=after,
+            device_id_type=pl.DeviceIdType.MESH,
+        ),
+    ]
+
     def send_halo():
-        for copy in (halos[BATCH], *halos[:BATCH]):
+        for copy in halos:
             copy.start()
 
     pl.when(has_next)(send_halo)
@@ -364,7 +361,7 @@
         gate_hi, gate_lo = split_two(jnp.broadcast_to(jnp.exp(ends[m]), (16, DSTATE)))
         gate_parts.append((dot(pick, gate_hi, plain), dot(pick, gate_lo, plain)))
     convolve(0)
-    pl.when(has_prior)(halos[BATCH].wait_recv)
+    pl.when(has_prior)(halos[0].wait_recv)
     doc_before = jnp.where(has_prior, doc_halo[...].astype(F32), -1.0)
     row8 = lax.broadcasted_iota(jnp.int32, (HALO, 128), 0)
 
@@ -406,7 +403,8 @@
     for m in range(BATCH):
         if m > 0:
             convolve(m)
-        pl.when(has_prior)(halos[m].wait_recv)
+        else:
+            pl.when(has_prior)(halos[1].wait_recv)
         same = [None, *(edge_mask(m, k) for k in range(1, TAPS))]
         scaled = []
         for j in range(tiles):
@@ -545,13 +543,10 @@
     plane_total(0)
     plane_total(1)
     scores_of(1)
-    inner_of(1)
     pl.when(goes(3))(lambda: pl.semaphore_wait(word.at[1], 1))
     two_planes(0)
     two_planes(1)
-    gate_inputs(1)
-    gate_both(1)
-    turn_weights()
+    inner_of(1)
     c_copies = []
     for m in range(BATCH):
         pl.when(has_below)(b_copies[m][1].wait_recv)
@@ -569,6 +564,10 @@
             copy.start()
         c_copies.append([all_of(m, hsend, c_send, c_recv)])
         hstate[m, home] = hsend[m, rank]
+        if m == 0:
+            gate_inputs(1)
+            gate_both(1)
+            turn_weights()
 
     quarter = plan.out // QUARTERS
 
@@ -793,8 +792,8 @@
         pltpu.VMEM((BATCH, 1, LENGTH), F32),
         pltpu.VMEM((BATCH, 2, plan.far, 1, LENGTH), F32),
         dma((9,)),
-        dma((BATCH + 1,)),
-        dma((BATCH + 1,)),
+        dma((2,)),
+        dma((2,)),
         dma((BATCH,)),
         dma((BATCH,)),
         dma((BATCH, 3)),

time: 55.6 us -> 54.9 us (0.987)
  no operation moved by 1% of the time
where the time goes in v11:
time: 54.9 us; the launch traced here: 54.7 us
  Pallas kernels  54 us (98%)
  local copies, waits for them, and re-layouts  0.73 us (1%)
    pallas_call x1, Pallas kernels, shards(): pl.pallas_call(functools.partial(layer_kernel, plan), name='mixer_layer',...  54 us

profile of v11, /device:TPU:449, one launch (start us, length us, event | category | flops | bytes accessed | tf_op | source)
XLA Modules:
  0.0 54.7 jit_solution(10125988330181624020)
XLA Ops:
  0.0 54.0 %mixer_layer.1 = bf16[2,320,256]{2,1,0:T(8,128)(2,1)S(1)} custom-call(bf16[2,256,640]{2,1,0:T(8,128)(2,1)} %x_hbm.1, bf16[2,256,640]{2,1,0:T(8,128)(2,1)} %z_hbm.1, bf16[2,256,128]{2,1,0:T(8,128)(2,1)} %b_hbm.1, bf16[2,256,128]{2,1,0:T(8,128)(2,1)} %c_hbm.1, f32[10,2,256]{2,1,0:T(2,128)} %bitcast.3, s32[2,256]{1,0:T(2,128)} %doc_hbm.1, ...), custom_call_target="tpu_custom_call" | custom-call | tf_op jit(solution)/shard_map/mixer_layer/pallas_call | solution.py:810
  54.0 0.7 %copy.15 = bf16[2,256,320]{1,2,0:T(8,128)(2,1)} copy(bf16[2,256,320]{1,2,0:T(8,128)(2,1)S(1)} %bitcast.2) | data formatting | bytes 655360

commit v12 on v11

--- a/solution.py
+++ b/solution.py
@@ -156,33 +156,6 @@
     up = {"mp": lax.rem(me + 1, members)}
     down = {"mp": lax.rem(me + members - 1, members)}
 
-    has_next, has_prior = place + 1 < blocks, place > 0
-
-    def one(flag):
-        return jnp.where(flag, 1, 0)
-
-    barrier = pltpu.get_barrier_semaphore()
-
-    def greet(peer):
-        pl.semaphore_signal(barrier, inc=1, device_id=peer, device_id_type=pl.DeviceIdType.MESH)
-
-    for k in range(1, ring):
-        greet(in_plane(lax.rem(rank + k, ring)))
-    greet(up)
-    greet(down)
-    pl.when(has_prior)(lambda: greet(prior))
-    count = ring - 1 + 2 + one(has_next)
-    above, below = {"sz": iz + 1}, {"sz": iz - 1}
-    has_above, has_below = iz + 1 < plan.planes, iz > 0
-    pl.when(has_below)(lambda: greet(below))
-    pl.when(has_above)(lambda: greet(above))
-    count = count + one(has_above) + one(has_below)
-
-    def tell_below(at):
-        pl.semaphore_signal(
-            word.at[at], inc=1, device_id=below, device_id_type=pl.DeviceIdType.MESH
-        )
-
     loads = []
 
     def load(src, dst, sem=None):
@@ -229,6 +202,33 @@
         taps,
     )
     got_gain = load(gain_hbm, gain_ref)
+
+    has_next, has_prior = place + 1 < blocks, place > 0
+
+    def one(flag):
+        return jnp.where(flag, 1, 0)
+
+    barrier = pltpu.get_barrier_semaphore()
+
+    def greet(peer):
+        pl.semaphore_signal(barrier, inc=1, device_id=peer, device_id_type=pl.DeviceIdType.MESH)
+
+    for k in range(1, ring):
+        greet(in_plane(lax.rem(rank + k, ring)))
+    greet(up)
+    greet(down)
+    pl.when(has_prior)(lambda: greet(prior))
+    count = ring - 1 + 2 + one(has_next)
+    above, below = {"sz": iz + 1}, {"sz": iz - 1}
+    has_above, has_below = iz + 1 < plan.planes, iz > 0
+    pl.when(has_below)(lambda: greet(below))
+    pl.when(has_above)(lambda: greet(above))
+    count = count + one(has_above) + one(has_below)
+
+    def tell_below(at):
+        pl.semaphore_signal(
+            word.at[at], inc=1, device_id=below, device_id_type=pl.DeviceIdType.MESH
+        )
 
     need(got_docs)
     need(got_rows)
@@ -494,7 +494,7 @@
         return pltpu.make_async_remote_copy(
             src_ref=source.at[m],
             dst_ref=brecv.at[m, slot],
-            send_sem=b_send.at[m, slot],
+            send_sem=b_send.at[slot],
             recv_sem=b_recv.at[m, slot],
             device_id={"sz": iz + k},
             device_id_type=pl.DeviceIdType.MESH,
@@ -729,9 +729,18 @@
                     device_id=to,
                     device_id_type=pl.DeviceIdType.MESH,
                 ).wait_send()
-    for m in range(BATCH):
-        for slot, k in jumps:
-            pl.when(goes(k))(b_copies[m][slot].wait_send)
+    for slot, k in jumps:
+        source = tsend if slot == 0 else usend
+        pl.when(goes(k))(
+            pltpu.make_async_remote_copy(
+                src_ref=source,
+                dst_ref=source,
+                send_sem=b_send.at[slot],
+                recv_sem=b_recv.at[0, slot],
+                device_id={"sz": iz + k},
+                device_id_type=pl.DeviceIdType.MESH,
+            ).wait_send
+        )
 
 
 def shards(
@@ -796,7 +805,7 @@
         dma((2,)),
         dma((BATCH,)),
         dma((BATCH,)),
-        dma((BATCH, 3)),
+        dma((3,)),
         dma((BATCH, 3)),
         dma((BATCH,)),
         dma((BATCH,)),

time: 54.9 us -> 54.9 us (level)
  no operation moved by 1% of the time
where the time goes in v12:
time: 54.9 us; the launch traced here: 54.8 us
  Pallas kernels  54 us (98%)
  local copies, waits for them, and re-layouts  0.73 us (1%)
    pallas_call x1, Pallas kernels, shards(): pl.pallas_call(functools.partial(layer_kernel, plan), name='mixer_layer',...  54 us

profile of v12, /device:TPU:449, one launch (start us, length us, event | category | flops | bytes accessed | tf_op | source)
XLA Modules:
  0.0 54.8 jit_solution(16048799764230000110)
XLA Ops:
  0.0 54.0 %mixer_layer.1 = bf16[2,320,256]{2,1,0:T(8,128)(2,1)S(1)} custom-call(bf16[2,256,640]{2,1,0:T(8,128)(2,1)} %x_hbm.1, bf16[2,256,640]{2,1,0:T(8,128)(2,1)} %z_hbm.1, bf16[2,256,128]{2,1,0:T(8,128)(2,1)} %b_hbm.1, bf16[2,256,128]{2,1,0:T(8,128)(2,1)} %c_hbm.1, f32[10,2,256]{2,1,0:T(2,128)} %bitcast.3, s32[2,256]{1,0:T(2,128)} %doc_hbm.1, ...), custom_call_target="tpu_custom_call" | custom-call | tf_op jit(solution)/shard_map/mixer_layer/pallas_call | solution.py:819
  54.0 0.7 %copy.15 = bf16[2,256,320]{1,2,0:T(8,128)(2,1)} copy(bf16[2,256,320]{1,2,0:T(8,128)(2,1)S(1)} %bitcast.2) | data formatting | bytes 655360
